TPU v7x, 256 devices: a whole 4x4x8 slice. The times are simulated.
256 devices in a mesh: vpair: 16 (over x, y), rank: 16 (over z, core).
Axes of the slice: x: 4, y: 4, z: 8, core: 2. Of those that a mesh axis runs over, the one named last changes fastest.
Arguments:
- amplitudes: bfloat16 [8, 1200, 1200], P(None, 'vpair', 'rank'), may hold values from -6 to 6
- factors: bfloat16 [1200, 8192], P('vpair', 'rank'), may hold values from -0.1875 to 0.1875
- kernel: bfloat16 [8192, 8192], P('vpair', 'rank'), may hold values from -0.875 to 0.875
- other_terms: float32 [8, 1200, 1200], P(None, 'vpair'), may hold values from -6 to 6
- virt_energy: float32 [1200], replicated, may hold values from 0.2 to 4
- pair_energy: float32 [8], replicated, may hold values from -3 to -0.5
Outputs:
- residual: float32 [8, 1200, 1200], P(None, 'vpair')
- update_rms: float32 [], replicated
All inputs are finite; a program needn't handle non-finite values.
Results may differ from a plain program's by a relative error of at most 0.0035.
Values may be sent and summed in bfloat16 or wider, within the bound.
A program may use at most 192 MiB of HBM per device.

v0:
```python
import jax
import jax.numpy as jnp
from jax import lax
from jax.sharding import Mesh
from jax.sharding import PartitionSpec as P

VPAIR = ("vpair_0", "vpair_1")


epsilon = 1e-06


def sent_to_all(shard, axis):
    copies = jnp.broadcast_to(shard, (lax.axis_size(axis), *shard.shape))
    return lax.all_to_all(copies, axis, split_axis=0, concat_axis=0, tiled=True)


def in_order(tiles, dim):
    lengths = list(tiles.shape[1:])
    lengths[dim] *= tiles.shape[0]
    return jnp.moveaxis(tiles, 0, dim).reshape(lengths)


def collect(shard, axis, dim):
    tiles = sent_to_all(shard, axis)
    return in_order(tiles, dim)


def filled_up(lines, count):
    spare = -len(lines) % count
    return jnp.pad(lines, [(0, spare)] + [(0, 0)] * (lines.ndim - 1))


def total_of(shard, axis):
    lines = shard.reshape(-1, *shard.shape[1:][-1:])
    padded = filled_up(lines, lax.axis_size(axis))
    own = lax.psum_scatter(padded, axis, scatter_dimension=0, tiled=True)
    whole = lax.all_gather(own, axis, axis=0, tiled=True)
    return whole[: len(lines)].reshape(shard.shape)


def one_axis_at_a_time(shard, axes):
    for axis in axes:
        shard = lax.psum(shard, axis)
    return shard


def shards(amplitudes, factors, kernel, other_terms, virt_energy, pair_energy):
    vpair_count = lax.axis_size(VPAIR)
    pair_count = amplitudes.shape[0]
    row_block = amplitudes.shape[1]
    virt_count = row_block * vpair_count
    right_block = kernel.shape[1]
    factor_rows = collect(factors, "rank", 1)
    factor_full = lax.all_gather(factor_rows, VPAIR, axis=0, tiled=True)
    factor_cols = lax.dynamic_slice_in_dim(
        factor_full, lax.axis_index("rank") * right_block, right_block, 1
    )
    half_done = jnp.einsum(
        "ons,sh->onh",
        collect(amplitudes, "rank", 2),
        factor_cols,
        preferred_element_type=jnp.float32,
    ).astype(jnp.bfloat16)
    kernel_sub = lax.all_to_all(kernel, VPAIR, split_axis=1, concat_axis=0, tiled=True).astype(
        jnp.float32
    )
    coupled = jnp.einsum(
        "cp,icq->ipq",
        factor_full,
        lax.all_to_all(half_done, VPAIR, split_axis=2, concat_axis=1, tiled=True),
        preferred_element_type=jnp.float32,
    )
    weighted = (kernel_sub[None] * coupled).astype(jnp.bfloat16)
    ladder_half = jnp.einsum(
        "ap,ipq->iaq", factor_full, weighted, preferred_element_type=jnp.float32
    ).astype(jnp.bfloat16)
    back_half = lax.all_to_all(ladder_half, VPAIR, split_axis=1, concat_axis=2, tiled=True)
    partial_value = jnp.einsum(
        "iaq,bq->iab", back_half, factor_cols, preferred_element_type=jnp.float32
    )
    row_energy = lax.dynamic_slice_in_dim(
        virt_energy, lax.axis_index(VPAIR) * row_block, row_block, 0
    )
    ladder = total_of(partial_value, "rank")
    residual = other_terms + ladder
    denominator = (
        row_energy[None, :, None] + virt_energy[None, None, :] - pair_energy[:, None, None]
    )
    update = residual / denominator
    squares = one_axis_at_a_time(jnp.sum(update * update), VPAIR)
    update_rms = jnp.sqrt(squares / (pair_count * virt_count * virt_count) + epsilon)
    return (residual, update_rms)


def solution(mesh):
    torus = Mesh(mesh.devices.reshape(4, 4, mesh.shape["rank"]), ("vpair_0", "vpair_1", "rank"))
    return jax.shard_map(
        shards,
        mesh=torus,
        in_specs=(
            P(None, VPAIR, "rank"),
            P(VPAIR, "rank"),
            P(VPAIR, "rank"),
            P(None, VPAIR, None),
            P(),
            P(),
        ),
        out_specs=(P(None, VPAIR, None), P()),
        check_vma=False,
    )
```

profile of v0, /device:TPU:1, one launch (start us, length us, event | category | flops | bytes accessed | tf_op | source)
XLA Modules:
  0.0 426.1 jit_solution(5133619606905226404)
XLA Ops:
  7.2 0.0 all-gather.5.cloned.1.call-start
  7.2 1.0 broadcast_in_dim.4
  8.2 43.8 %all_to_all.56 = bf16[16,75,512]{2,1,0:T(8,128)(2,1)S(1)} all-to-all(bf16[16,75,512]{2,1,0:T(8,128)(2,1)S(1)} %broadcast_in_dim.4), channel_id=1, replica_groups=mesh['vpair_0'=4,'vpair_1'=4,'rank'=16] {'rank'}, dimensions={0} | all-to-all | bytes 2457600 | tf_op jit(solution)/shard_map/all_to_all | solution.py:15
  52.0 0.7 copy.30
  52.7 1.7 reshape.63
  54.4 1.8 broadcast_in_dim.5
  56.2 3.6 all-to-all-start.2
  59.8 1.0 copy.28
  60.8 54.8 %all-to-all-done.2 = bf16[16,8,75,75]{3,1,2,0:T(8,128)(2,1)S(1)} async-done(((bf16[16,8,75,75]{3,1,2,0:T(8,128)(2,1)}), bf16[16,8,75,75]{3,1,2,0:T(8,128)(2,1)S(1)}, u32[]{:S(2)}, u32[]{:S(2)}) %all-to-all-start.2) | async-done | bytes 1440032 | tf_op jit(solution)/shard_map/all_to_all | solution.py:15
  115.6 6.7 %all-to-all-start = ((bf16[512,16,32]{0,2,1:T(8,128)(2,1)}), bf16[512,16,32]{0,2,1:T(8,128)(2,1)S(1)}, u32[]{:S(2)}, u32[]{:S(2)}) async-start(bf16[512,16,32]{0,2,1:T(8,128)(2,1)} %bitcast), calls=%async_computation | async-start | bytes 1048576 | tf_op jit(solution)/shard_map/all_to_all | solution.py:65
  122.3 1.8 copy.40
  124.0 4.2 reshape.70
  128.3 66.2 %all-gather.5.cloned.1.call-done = bf16[16,75,8192]{2,1,0:T(8,128)(2,1)} async-done(((bf16[1,75,8192]{2,1,0:T(8,128)(2,1)}), bf16[16,75,8192]{2,1,0:T(8,128)(2,1)}) %all-gather.5.cloned.1.call-update) | async-done | bytes 19660816 | tf_op jit(solution)/shard_map/all_gather | solution.py:55
  194.5 22.4 %reshape.64 = bf16[1200,8192]{1,0:T(8,128)(2,1)} reshape(bf16[16,75,8192]{2,1,0:T(8,128)(2,1)} %all-gather.5.cloned.1.call-done) | data formatting | bytes 39321600
  216.9 2.3 fusion.4
  219.2 1.5 copy.33
  220.7 5.0 %all-to-all-start.3 = ((bf16[8,75,512]{1,0,2:T(8,128)(2,1)}), bf16[8,75,512]{1,0,2:T(8,128)(2,1)S(1)}, u32[]{:S(2)}, u32[]{:S(2)}) async-start(bf16[8,75,512]{1,0,2:T(8,128)(2,1)} %copy.33), calls=%async_computation.3 | async-start | bytes 2097152 | tf_op jit(solution)/shard_map/all_to_all | solution.py:71
  225.7 0.2 all-gather.7.cloned.1.call-start
  225.9 0.1 convert_bitcast_fusion
  226.1 0.1 copy.43
  226.2 22.3 %reshape.69 = bf16[1200,8192,1]{1,0,2:T(8,128)(2,1)} reshape(bf16[16,75,8192]{2,1,0:T(8,128)(2,1)} %all-gather.5.cloned.1.call-done) | data formatting | bytes 39321600
  248.5 0.7 copy.35
  249.2 1.3 all_to_all.47
  250.5 17.8 %fusion.3 = bf16[8,1200,32]{1,2,0:T(8,128)(2,1)} fusion(bf16[1200,8192,1]{1,0,2:T(8,128)(2,1)} %reshape.69, bf16[8,1200,32]{1,2,0:T(8,128)(2,1)S(1)} %all_to_all.47, f32[8192,32]{0,1:T(8,128)S(1)} %bitcast.57), kind=kOutput, calls=%fused_computation.6 | convolution fusion | flops 10070831104 | bytes 21938176 | tf_op jit(solution)/shard_map/ap,ipq->iaq/dot_general | solution.py:75
  268.3 3.9 copy.36
  272.2 2.4 reshape.73
  274.7 17.1 %all_to_all.57 = bf16[16,2,9600]{2,1,0:T(2,128)(2,1)} all-to-all(bf16[16,2,9600]{2,1,0:T(2,128)(2,1)S(1)} %reshape.73), channel_id=1, replica_groups=mesh['vpair_0'=4,'vpair_1'=4,'rank'=16] {'vpair_0','vpair_1'}, dimensions={0} | all-to-all | bytes 1228800 | tf_op jit(solution)/shard_map/all_to_all | solution.py:78
  291.8 3.6 reshape.74
  295.4 2.8 copy.37
  298.2 0.8 dot_general.17
  299.0 2.4 fusion.6
  301.4 0.2 pad.4
  301.6 33.1 %fusion = f32[40,1200]{1,0:T(8,128)S(1)} fusion(f32[608,1200]{1,0:T(8,128)S(1)} %pad.4), kind=kCustom, calls=%all-reduce-scatter | all-reduce-scatter fusion | flops 768001 | bytes 3111424
  334.7 3.4 collective-permute-start
  338.2 0.6 dynamic-slice.4
  339.4 1.4 collective-permute-done
  340.8 0.2 concatenate
  341.0 0.7 dynamic-slice_bitcast_fusion
  341.8 0.1 dynamic_slice.7
  341.9 0.9 broadcast_add_fusion
  342.7 40.5 %all-gather.7.cloned.1.call-done = f32[16,38,1200]{2,1,0:T(8,128)} async-done(((f32[1,38,1200]{2,1,0:T(8,128)}), f32[16,38,1200]{2,1,0:T(8,128)}) %all-gather.7.cloned.1.call-update) | async-done | bytes 2918416 | tf_op jit(solution)/shard_map/all_gather | solution.py:38
  383.2 2.1 reshape.66
  385.4 1.8 slice.4
  387.2 3.9 reshape.61
  391.2 4.8 %multiply_reduce_fusion = (f32[]{:T(128)}, f32[8,75,1200]{2,1,0:T(8,128)S(1)}) fusion(f32[8]{0:T(128)S(1)} %copy-done.3, f32[75,1200]{1,0:T(8,128)} %broadcast_add_fusion, f32[8,75,1200]{2,1,0:T(8,128)} %reshape.61, f32[8,75,1200]{2,0,1:T(8,128)} %param.9), kind=kLoop, calls=%fused_computation.4 | loop fusion | flops 3599999 | bytes 9000036 | tf_op jit(solution)/shard_map/reduce_sum | solution.py:91
  395.9 9.0 %psum.14 = f32[]{:T(128)} all-reduce(f32[]{:T(128)} %get-tuple-element.8), channel_id=1, replica_groups=mesh['vpair_0'=4,'vpair_1'=4,'rank'=16] {'vpair_0'}, use_global_device_ids=true, to_apply=%region_2.3 | all-reduce | flops 1 | bytes 8 | tf_op jit(solution)/shard_map/psum | solution.py:44
  404.9 3.4 copy.39
  408.3 9.1 %psum.15 = f32[]{:T(128)} all-reduce(f32[]{:T(128)} %psum.14), channel_id=1, replica_groups=mesh['vpair_0'=4,'vpair_1'=4,'rank'=16] {'vpair_1'}, use_global_device_ids=true, to_apply=%region_3.4 | all-reduce | flops 1 | bytes 8 | tf_op jit(solution)/shard_map/psum | solution.py:44
  (15 shorter events, 0.1 us)
Async XLA Ops:
  7.2 187.3 %all-gather.5.cloned.1.call-start = ((), (), s32[]{:S(2)}) async-start(), calls=%async_computation.5 | async-start | bytes 22282240 | tf_op jit(solution)/shard_map/all_gather | solution.py:55
  52.0 2.4 copy-start.1
  54.4 5.4 %copy-start = (bf16[512,512]{1,0:T(8,128)(2,1)S(1)}, bf16[512,512]{1,0:T(8,128)(2,1)}, u32[]{:S(2)}) copy-start(bf16[512,512]{1,0:T(8,128)(2,1)} %param.8) | copy-start | bytes 1572868
  56.2 59.4 %all-to-all-start.2 = ((bf16[16,8,75,75]{3,1,2,0:T(8,128)(2,1)}), bf16[16,8,75,75]{3,1,2,0:T(8,128)(2,1)S(1)}, u32[]{:S(2)}, u32[]{:S(2)}) async-start(bf16[16,8,75,75]{3,1,2,0:T(8,128)(2,1)} %broadcast_in_dim.5), calls=%async_computation.2 | async-start | bytes 4915200 | tf_op jit(solution)/shard_map/all_to_all | solution.py:15
  115.6 105.1 %all-to-all-start = ((bf16[512,16,32]{0,2,1:T(8,128)(2,1)}), bf16[512,16,32]{0,2,1:T(8,128)(2,1)S(1)}, u32[]{:S(2)}, u32[]{:S(2)}) async-start(bf16[512,16,32]{0,2,1:T(8,128)(2,1)} %bitcast), calls=%async_computation | async-start | bytes 1048576 | tf_op jit(solution)/shard_map/all_to_all | solution.py:65
  220.7 27.8 %all-to-all-start.3 = ((bf16[8,75,512]{1,0,2:T(8,128)(2,1)}), bf16[8,75,512]{1,0,2:T(8,128)(2,1)S(1)}, u32[]{:S(2)}, u32[]{:S(2)}) async-start(bf16[8,75,512]{1,0,2:T(8,128)(2,1)} %copy.33), calls=%async_computation.3 | async-start | bytes 2097152 | tf_op jit(solution)/shard_map/all_to_all | solution.py:71
  225.7 157.5 %all-gather.7.cloned.1.call-start = ((), (), s32[]{:S(2)}) async-start(), calls=%async_computation.6 | async-start | bytes 3481600 | tf_op jit(solution)/shard_map/all_gather | solution.py:38
  301.6 36.6 %copy-start.4 = (u32[256]{0:T(256)S(1)}, u32[256]{0:T(256)}, u32[]{:S(2)}) copy-start(u32[256]{0:T(256)} %constant.40) | copy-start | bytes 3076
  301.6 40.2 %copy-start.2 = (f32[1200]{0:T(1024)S(1)}, f32[1200]{0:T(1024)}, u32[]{:S(2)}) copy-start(f32[1200]{0:T(1024)} %param.10) | copy-start | bytes 14404
  334.7 6.1 %collective-permute-start = (f32[30,1200]{1,0:T(8,128)S(1)}, f32[30,1200]{1,0:T(8,128)S(1)}, u32[]{:S(2)}, u32[]{:S(2)}) collective-permute-start(f32[30,1200]{1,0:T(8,128)S(1)} %slice.5), channel_id=1, source_target_pairs={{0,1},{1,2},{2,3},{3,4},{4,5},{5,6},{6,7},{7,8},{8,9},{9,10},{10,1... | collective-permute-start | bytes 432008
  387.2 3.9 copy-start.3
Sparse Core Ops, SparseCore 0:
  54.5 139.8 all-gather.4
  341.9 41.3 all-gather.6
where the time goes:
time: 429 us; the launch traced here: 426 us
  waiting for transfers between devices  163 us (38%)
  blocking collectives  112 us (26%)
  local copies, waits for them, and re-layouts  87.1 us (20%)
  matrix products  22.5 us (5%)
  starting transfers between devices  18.9 us (4%)
  between operations  16.8 us (4%)
  other arithmetic  5.74 us (1%)
    all_gather x1, waiting for transfers between devices, shards(): factor_full = lax.all_gather(factor_rows, VPAIR, axis=0, tiled=True)  66.2 us
    unnamed x22, local copies, waits for them, and re-layouts  60.5 us
    all_to_all x1, waiting for transfers between devices, sent_to_all(): return lax.all_to_all(copies, axis, split_axis=0, concat_axis=0, tiled=True)  54.8 us
    all_to_all x1, blocking collectives, sent_to_all(): return lax.all_to_all(copies, axis, split_axis=0, concat_axis=0, tiled=True)  43.8 us
    all_gather x1, waiting for transfers between devices, total_of(): whole = lax.all_gather(own, axis, axis=0, tiled=True)  40.5 us
    unnamed x1, blocking collectives  33.1 us
    psum x2, blocking collectives, one_axis_at_a_time(): shard = lax.psum(shard, axis)  18.1 us
    dot_general x1, matrix products, shards(): jnp.einsum('ap,ipq->iaq', factor_full, weighted, preferred_element_type=j...  17.8 us
  transfers between devices with their start and end apart: 6, of which 4 were waited for; matrix products, arithmetic and copies ran while one was open for 14% of the time, Pallas kernels for 0%

commit v1 on v0

v1 whole, which is shorter than its diff:
```python
import functools

import jax
import jax.numpy as jnp
from jax import lax
from jax.experimental import pallas as pl
from jax.experimental.pallas import tpu as pltpu
from jax.sharding import Mesh
from jax.sharding import PartitionSpec as P

MESH = pl.DeviceIdType.MESH
BF = jnp.bfloat16
F32 = jnp.float32
EPS = 1e-06
NT = (((1,), (1,)), ((), ()))
TN = (((0,), (0,)), ((), ()))
TICKS = 12
READY = 6


def roll(a, shift):
    shift %= 128
    return a if shift == 0 else pltpu.roll(a, shift, 1)


def ladder_kernel(
    f_ref, t_ref, zt_ref, other_ref, ea_ref, eb_ref, ep_ref, out_ref, rms_ref,
    xb, tt, ttp, half, hs, hb, ht, zb_ref, wt, acc, rb, bs, br, ls, lb, lt, ltr, lc, la, sc, sp, sz,
    x_ss, x_rs, c_ss, c_rs, r_ss, r_rs, t_ss, t_rs, u_ss, u_rs, g_ss, g_rs, m_ss, m_rs, loc,
):
    x, y, z, c = (lax.axis_index(n) for n in ("x", "y", "z", "core"))
    v = 4 * x + y
    xp, xm = (x + 1) % 4, (x + 3) % 4
    yp, ym = (y + 1) % 4, (y + 3) % 4
    zp, zm = (z + 1) % 8, (z + 7) % 8
    sib = {"core": 1 - c}

    def rows(i, off, n, ref=None):
        return (xb if ref is None else ref).at[i, pl.ds(pl.multiple_of(off, 16), n)]

    def send(src, dst, ss, rs, dev):
        pltpu.make_async_remote_copy(
            src_ref=src, dst_ref=dst, send_sem=ss, recv_sem=rs, device_id=dev, device_id_type=MESH
        ).start()

    def got(dst, rs):
        pltpu.make_async_remote_copy(
            src_ref=dst, dst_ref=dst, send_sem=rs, recv_sem=rs, device_id=sib, device_id_type=MESH
        ).wait_recv()

    def left(src, ss):
        pltpu.make_async_remote_copy(
            src_ref=src, dst_ref=src, send_sem=ss, recv_sem=ss, device_id=sib, device_id_type=MESH
        ).wait_send()

    def a_off(i, j):
        return i * 128 + j * 32

    def b_off(i, j):
        return 512 + j * 128 + i * 32

    def c_off(i, j):
        return 1024 + i * 64 + j * 16

    own = [
        pltpu.make_async_copy(f_ref.at[pl.ds(0, 32)], rows(z, a_off(x, y), 32), loc.at[0]),
        pltpu.make_async_copy(f_ref.at[pl.ds(32, 32)], rows(z, b_off(x, y), 32), loc.at[1]),
        pltpu.make_async_copy(f_ref.at[pl.ds(64, 16)], rows(z, c_off(x, y), 16), loc.at[2]),
        pltpu.make_async_copy(t_ref, tt.at[2 * z + c], loc.at[3]),
    ]
    for o in own:
        o.start()

    bar = pltpu.get_barrier_semaphore()

    def plane_dev(j, core):
        w = (v + j) % 16
        return {"x": w // 4, "y": w % 4, "core": core}

    def greet(j, _):
        pl.semaphore_signal(bar, inc=1, device_id=plane_dev(j, c), device_id_type=MESH)
        pl.semaphore_signal(bar, inc=1, device_id=plane_dev(j, 1 - c), device_id_type=MESH)
        return 0

    lax.fori_loop(1, 16, greet, 0)
    pl.semaphore_signal(bar, inc=1, device_id=sib, device_id_type=MESH)

    def greet_z(j, _):
        pl.semaphore_signal(bar, inc=1, device_id={"z": (z + j) % 8}, device_id_type=MESH)
        return 0

    lax.fori_loop(1, 8, greet_z, 0)
    for o in own:
        o.wait()
    pl.semaphore_wait(bar, 38)

    def zblk(k):
        return (z + ((k + 1) // 2) * (2 * (k % 2) - 1) + 8) % 8

    def ring_step(s, zl, zr):
        for d, (blk, dev) in enumerate(((zl, zp), (zr, zm))):
            i = 2 * s + d
            dev = {"z": dev}
            r = 2 * blk + c
            if s < 3:
                for o in (a_off(x, y), b_off(x, y)):
                    w = 0 if o is None else o
                send(rows(blk, a_off(x, y), 32), rows(blk, a_off(x, y), 32), r_ss.at[i], r_rs.at[i], dev)
                send(rows(blk, b_off(x, y), 32), rows(blk, b_off(x, y), 32), r_ss.at[8 + i], r_rs.at[8 + i], dev)
                send(tt.at[r], tt.at[r], t_ss.at[i], t_rs.at[i], dev)
            elif d == 0:
                send(rows(blk, a_off(x, y), 32), rows(blk, a_off(x, y), 32), r_ss.at[i], r_rs.at[i], dev)
                send(tt.at[r, pl.ds(0, 48)], tt.at[r, pl.ds(0, 48)], t_ss.at[i], t_rs.at[i], dev)
            else:
                send(rows(blk, b_off(x, y), 32), rows(blk, b_off(x, y), 32), r_ss.at[i], r_rs.at[i], dev)
                send(tt.at[r, pl.ds(48, 32)], tt.at[r, pl.ds(48, 32)], t_ss.at[i], t_rs.at[i], dev)

    def push_t(n, blk):
        r = 2 * blk + c
        send(tt.at[r], tt.at[r], u_ss.at[n], u_rs.at[n], sib)

    def ring_got(s):
        lo, hi = (z + 7 - s) % 8, (z + 1 + s) % 8
        for d, blk in enumerate((lo, hi)):
            i = 2 * s + d
            r = 2 * blk + c
            if s < 3:
                got(rows(blk, a_off(x, y), 32), r_rs.at[i])
                got(rows(blk, b_off(x, y), 32), r_rs.at[8 + i])
                got(tt.at[r], t_rs.at[i])
            elif d == 0:
                got(rows(blk, a_off(x, y), 32), r_rs.at[i])
                got(tt.at[r, pl.ds(0, 48)], t_rs.at[i])
            else:
                got(rows(blk, b_off(x, y), 32), r_rs.at[i])
                got(tt.at[r, pl.ds(48, 32)], t_rs.at[i])
        return lo, hi

    ring_step(0, z, z)
    push_t(0, z)

    def c_piece(i, j, h):
        return xb.at[z, pl.ds(pl.multiple_of(c_off(i, j), 16), 16), pl.ds(256 * h, 256)]

    def c_step(s):
        if s == 0:
            p = rows(z, c_off(x, y), 16)
            send(p, p, c_ss.at[0], c_rs.at[0], {"y": yp})
            send(p, p, c_ss.at[1], c_rs.at[1], {"y": ym})
        elif s == 1:
            got(rows(z, c_off(x, ym), 16), c_rs.at[0])
            got(rows(z, c_off(x, yp), 16), c_rs.at[1])
            p, q = c_piece(x, ym, 0), c_piece(x, yp, 1)
            send(p, p, c_ss.at[2], c_rs.at[2], {"y": yp})
            send(q, q, c_ss.at[3], c_rs.at[3], {"y": ym})
        elif s == 2:
            got(c_piece(x, (y + 2) % 4, 0), c_rs.at[2])
            got(c_piece(x, (y + 2) % 4, 1), c_rs.at[3])
            p = rows(z, c_off(x, 0), 64)
            send(p, p, c_ss.at[4], c_rs.at[4], {"x": xp})
            send(p, p, c_ss.at[5], c_rs.at[5], {"x": xm})
        elif s == 3:
            got(rows(z, c_off(xm, 0), 64), c_rs.at[4])
            got(rows(z, c_off(xp, 0), 64), c_rs.at[5])
            p, q = rows(z, c_off(xm, 0), 32), rows(z, c_off(xp, 2), 32)
            send(p, p, c_ss.at[6], c_rs.at[6], {"x": xp})
            send(q, q, c_ss.at[7], c_rs.at[7], {"x": xm})
        else:
            if s == 4:
                got(rows(z, c_off((x + 2) % 4, 0), 32), c_rs.at[6])
                got(rows(z, c_off((x + 2) % 4, 2), 32), c_rs.at[7])
            else:
                g = s - 5
                lo, hi = (z + 7 - g) % 8, (z + 1 + g) % 8
                i = 8 + 2 * g
                if g < 3:
                    got(rows(lo, 1024, 256), c_rs.at[i])
                    got(rows(hi, 1024, 256), c_rs.at[i + 1])
                else:
                    got(rows(lo, 1024, 128), c_rs.at[i])
                    got(rows(hi, 1152, 128), c_rs.at[i + 1])
            if s < 8:
                h = s - 4
                i = 8 + 2 * h
                lo, hi = (z + 8 - h) % 8, (z + h) % 8
                n = 256 if h < 3 else 128
                o = 1024 if h < 3 else 1152
                send(rows(lo, 1024, n), rows(lo, 1024, n), c_ss.at[i], c_rs.at[i], {"z": zp})
                send(rows(hi, o, n), rows(hi, o, n), c_ss.at[i + 1], c_rs.at[i + 1], {"z": zm})

    def s1(k):
        b = zblk(k)
        p, q = rows(b, a_off(x, y), 32), rows(b, b_off(x, y), 32)
        send(p, p, x_ss.at[k, 0], x_rs.at[k, 0], {"y": yp})
        send(p, p, x_ss.at[k, 1], x_rs.at[k, 1], {"y": ym})
        send(q, q, x_ss.at[k, 8], x_rs.at[k, 8], {"x": xp})
        send(q, q, x_ss.at[k, 9], x_rs.at[k, 9], {"x": xm})

    def s2(k):
        b = zblk(k)
        got(rows(b, a_off(x, ym), 32), x_rs.at[k, 0])
        got(rows(b, a_off(x, yp), 32), x_rs.at[k, 1])
        p, q = rows(b, a_off(x, ym), 16), rows(b, a_off(x, yp) + 16, 16)
        send(p, p, x_ss.at[k, 2], x_rs.at[k, 2], {"y": yp})
        send(q, q, x_ss.at[k, 3], x_rs.at[k, 3], {"y": ym})
        got(rows(b, b_off(xm, y), 32), x_rs.at[k, 8])
        got(rows(b, b_off(xp, y), 32), x_rs.at[k, 9])
        p, q = rows(b, b_off(xm, y), 16), rows(b, b_off(xp, y) + 16, 16)
        send(p, p, x_ss.at[k, 10], x_rs.at[k, 10], {"x": xp})
        send(q, q, x_ss.at[k, 11], x_rs.at[k, 11], {"x": xm})

    def s3(k):
        b = zblk(k)
        y2, x2 = (y + 2) % 4, (x + 2) % 4
        got(rows(b, a_off(x, y2), 16), x_rs.at[k, 2])
        got(rows(b, a_off(x, y2) + 16, 16), x_rs.at[k, 3])
        p = rows(b, a_off(x, 0), 128)
        send(p, p, x_ss.at[k, 4], x_rs.at[k, 4], {"x": xp})
        send(p, p, x_ss.at[k, 5], x_rs.at[k, 5], {"x": xm})
        got(rows(b, b_off(x2, y), 16), x_rs.at[k, 10])
        got(rows(b, b_off(x2, y) + 16, 16), x_rs.at[k, 11])
        p = rows(b, b_off(0, y), 128)
        send(p, p, x_ss.at[k, 12], x_rs.at[k, 12], {"y": yp})
        send(p, p, x_ss.at[k, 13], x_rs.at[k, 13], {"y": ym})

    def s4(k):
        b = zblk(k)
        got(rows(b, a_off(xm, 0), 128), x_rs.at[k, 4])
        got(rows(b, a_off(xp, 0), 128), x_rs.at[k, 5])
        p, q = rows(b, a_off(xm, 0), 64), rows(b, a_off(xp, 2), 64)
        send(p, p, x_ss.at[k, 6], x_rs.at[k, 6], {"x": xp})
        send(q, q, x_ss.at[k, 7], x_rs.at[k, 7], {"x": xm})
        got(rows(b, b_off(0, ym), 128), x_rs.at[k, 12])
        got(rows(b, b_off(0, yp), 128), x_rs.at[k, 13])
        p, q = rows(b, b_off(0, ym), 64), rows(b, b_off(2, yp), 64)
        send(p, p, x_ss.at[k, 14], x_rs.at[k, 14], {"y": yp})
        send(q, q, x_ss.at[k, 15], x_rs.at[k, 15], {"y": ym})

    def s5(k):
        b = zblk(k)
        y2, x2 = (y + 2) % 4, (x + 2) % 4
        got(rows(b, a_off(x2, 0), 64), x_rs.at[k, 6])
        got(rows(b, a_off(x2, 2), 64), x_rs.at[k, 7])
        got(rows(b, b_off(0, y2), 64), x_rs.at[k, 14])
        got(rows(b, b_off(2, y2), 64), x_rs.at[k, 15])

    def send_kernel():
        kc = y % 2

        def one(j, _):
            w = (v + j) % 16
            src = zt_ref.at[pl.ds(pl.multiple_of(32 * w, 32), 32)]
            send(src, zb_ref.at[v // 2, c], m_ss.at[0], m_rs.at[0], plane_dev(j, kc))
            return 0

        lax.fori_loop(1, 16, one, 0)
        src = zt_ref.at[pl.ds(pl.multiple_of(32 * v, 32), 32)]

        @pl.when(c == kc)
        def _():
            pltpu.make_async_copy(src, zb_ref.at[v // 2, c], m_rs.at[0]).start()

        @pl.when(c != kc)
        def _():
            send(src, zb_ref.at[v // 2, c], m_ss.at[0], m_rs.at[0], sib)

    def make_half():
        for n in range(1, 8):
            b = zblk(n)
            got(tt.at[2 * b + 1 - c], u_rs.at[n])
        got(tt.at[2 * z + 1 - c], u_rs.at[0])
        for i in range(4):
            for j in range(4):
                w = 4 * i + j
                ttp[pl.ds(a_off(i, j), 32), :] = tt[w, pl.ds(0, 32), :]
                ttp[pl.ds(b_off(i, j), 32), :] = tt[w, pl.ds(32, 32), :]
                ttp[pl.ds(c_off(i, j), 16), :] = tt[w, pl.ds(64, 16), :]
        lanes = lax.broadcasted_iota(jnp.int32, (80, 128), 1) // 32

        def chunk(a, _):
            q = pl.ds(pl.multiple_of(256 * a, 256), 256)
            half[...] = lax.dot_general(ttp[...], xb[z, :, q], TN, preferred_element_type=F32)
            for h in range(2):
                for g in range(2):
                    part = [half[pl.ds(80 * (4 * g + k), 80), pl.ds(128 * h, 128)] for k in range(4)]
                    for s in range(4):
                        m = roll(part[0], (0 - s) * 32)
                        for k in range(1, 4):
                            m = jnp.where(lanes == k, roll(part[k], (k - s) * 32), m)
                        hs[8 * a + 4 * h + s, :, pl.ds(128 * g, 128)] = m.astype(BF)
            return 0

        lax.fori_loop(0, 2, chunk, 0)

        def one(j, _):
            send(hs.at[(v + j) % 16], hb.at[c, v], m_ss.at[1], m_rs.at[1], plane_dev(j, c))
            return 0

        lax.fori_loop(1, 16, one, 0)
        pltpu.make_async_copy(hs.at[v], hb.at[c, v], m_rs.at[1]).start()

    def take_half():
        got(hb.at[c], m_rs.at[1])
        send(hb.at[c], hb.at[c], m_ss.at[2], m_rs.at[2], sib)
        acc[...] = jnp.zeros_like(acc)
        got(hb.at[1 - c], m_rs.at[2])
        for s in range(2):
            to = pl.ds(256 * s, 256)
            for i in range(4):
                m = jnp.concatenate([hb[s, 4 * i + j, pl.ds(0, 32), :] for j in range(4)], 0)
                ht[to, pl.ds(128 * i, 128)] = m.astype(F32).T.astype(BF)
                m = jnp.concatenate([hb[s, 4 * j + i, pl.ds(32, 32), :] for j in range(4)], 0)
                ht[to, pl.ds(512 + 128 * i, 128)] = m.astype(F32).T.astype(BF)
            for i in range(2):
                m = jnp.concatenate([hb[s, 8 * i + j, pl.ds(64, 16), :] for j in range(8)], 0)
                ht[to, pl.ds(1024 + 128 * i, 128)] = m.astype(F32).T.astype(BF)
        got(zb_ref, m_rs.at[0])

    def compute(k, _):
        b = zblk(k)
        for q in range(2):
            q = pl.ds(256 * q, 256)
            cp = jnp.dot(ht[...], xb[b, :, q], preferred_element_type=F32)
            zz = zb_ref[b, :, :, q].astype(F32)
            for s in range(2):
                for i in range(8):
                    o = 256 * s + 32 * i
                    wt[pl.ds(o, 32), q] = (cp[o : o + 32] * zz[s]).astype(BF)
        for a in range(5):
            a = pl.ds(256 * a, 256)
            acc[:, a] += lax.dot_general(wt[...], xb[b, a, :], NT, preferred_element_type=F32)
        return 0

    def tick(t, _):
        for s in range(1, 9):
            if s <= 4:

                @pl.when(t == s)
                def _(s=s):
                    lo, hi = ring_got(s - 1)
                    if s < 4:
                        ring_step(s, lo, hi)
                        push_t(2 * s - 1, hi)
                        push_t(2 * s, lo)
                    else:
                        push_t(7, lo)

        @pl.when(t >= 4)
        def _():
            s5(t - 4)

        for s in range(9):

            @pl.when(t == s)
            def _(s=s):
                c_step(s)

        @pl.when((t >= 3) & (t < 11))
        def _():
            s4(t - 3)

        @pl.when((t >= 2) & (t < 10))
        def _():
            s3(t - 2)

        @pl.when((t >= 1) & (t < 9))
        def _():
            s2(t - 1)

        @pl.when(t < 8)
        def _():
            s1(t)

        @pl.when(t == 0)
        def _():
            send_kernel()

        @pl.when(t == 4)
        def _():
            make_half()

        @pl.when(t == READY)
        def _():
            take_half()

        lo = jnp.minimum(jnp.maximum(t - 4, 0), jnp.maximum(2 * (t - READY), 0))
        hi = jnp.minimum(jnp.maximum(t - 3, 0), jnp.maximum(2 * (t - READY + 1), 0))
        lax.fori_loop(lo, hi, compute, 0)
        return 0

    lax.fori_loop(0, TICKS, tick, 0)

    mine = pl.ds(pl.multiple_of(256 * c, 256), 256)
    give = acc.at[pl.ds(pl.multiple_of(256 * (1 - c), 256), 256)]
    send(give, rb, m_ss.at[3], m_rs.at[3], sib)
    got(rb, m_rs.at[3])
    for n in range(10):
        a = pl.ds(128 * n, 128)
        m = (acc[mine, a] + rb[:, a]).T.astype(BF)
        if n < 4:
            for j in range(4):
                bs[4 * n + j, pl.ds(0, 32), :] = m[32 * j : 32 * j + 32]
        elif n < 8:
            for j in range(4):
                bs[4 * j + n - 4, pl.ds(32, 32), :] = m[32 * j : 32 * j + 32]
        else:
            for j in range(8):
                bs[8 * (n - 8) + j, pl.ds(64, 16), :] = m[16 * j : 16 * j + 16]

    def give_back(j, _):
        send(bs.at[(v + j) % 16], br.at[v], m_ss.at[4], m_rs.at[4], plane_dev(j, c))
        return 0

    lax.fori_loop(1, 16, give_back, 0)
    pltpu.make_async_copy(bs.at[v], br.at[v], m_rs.at[4]).start()
    got(br, m_rs.at[4])

    lanes = lax.broadcasted_iota(jnp.int32, (80, 128), 1) // 32
    for g in range(2):
        for a in range(4):
            part = [br[4 * a + s, :, pl.ds(128 * g, 128)].astype(F32) for s in range(4)]
            for k in range(4):
                m = roll(part[0], (0 - k) * 32)
                for s in range(1, 4):
                    m = jnp.where(lanes == s, roll(part[s], (s - k) * 32), m)
                ls[4 * g + k, :, pl.ds(128 * a, 128)] = m.astype(BF)

    def give_z(j, _):
        w = (z + j) % 8
        send(ls.at[w], lb.at[z], m_ss.at[5], m_rs.at[5], {"z": w})
        return 0

    lax.fori_loop(1, 8, give_z, 0)
    pltpu.make_async_copy(ls.at[z], lb.at[z], m_rs.at[5]).start()
    got(lb, m_rs.at[5])

    lt[...] = jnp.zeros_like(lt)

    def lad(b, _):
        for a in range(5):
            a = pl.ds(256 * a, 256)
            lt[a, pl.ds(0, 80)] += lax.dot_general(xb[b, a, :], lb[b], NT, preferred_element_type=F32)
        return 0

    lax.fori_loop(0, 8, lad, 0)
    send(lt, ltr, m_ss.at[6], m_rs.at[6], sib)
    got(ltr, m_rs.at[6])
    lc[pl.ds(1200, 80), :] = jnp.zeros((80, 128), F32)
    for i in range(4):
        for j in range(4):
            o = 75 * (4 * i + j)
            for n, off, cnt in ((0, a_off(i, j), 32), (32, b_off(i, j), 32), (64, c_off(i, j), 11)):
                lc[pl.ds(o + n, cnt), :] = lt[pl.ds(off, cnt), :] + ltr[pl.ds(off, cnt), :]
    total = jnp.zeros((75, 128), F32)
    ep = ep_ref[z]
    for n in range(10):
        b = pl.ds(128 * n, 128)
        m = lc[b, :].T[:80]
        la[z, :, b] = m.astype(BF)
        w = 128 if n < 9 else 48
        b = pl.ds(128 * n, w)
        den = ea_ref[...] + eb_ref[:, b] - ep
        u = (other_ref[z, :, b] + m[:75, :w]) / den
        u = u * u
        if w < 128:
            u = jnp.concatenate([u, jnp.zeros((75, 128 - w), F32)], 1)
        total = total + u
    sc[...] = jnp.full((8, 128), jnp.sum(total), F32)

    def la_part(i, h, lo=0, n=80):
        return la.at[i, pl.ds(lo, n), pl.ds(pl.multiple_of(640 * h, 128), 640)]

    def la_step(s, lo, hi):
        for d, (blk, dev) in enumerate(((lo, zp), (hi, zm))):
            p = la_part(blk, c) if s < 3 else la_part(blk, c, 48 * d, 48 - 16 * d)
            send(p, p, g_ss.at[2 * s + d], g_rs.at[2 * s + d], {"z": dev})

    def la_push(n, blk):
        send(la_part(blk, c), la_part(blk, c), g_ss.at[8 + n], g_rs.at[8 + n], sib)

    la_step(0, z, z)

    def give_sum(j, _):
        send(sc, sp.at[v], m_ss.at[7], m_rs.at[7], plane_dev(j, c))
        return 0

    lax.fori_loop(1, 16, give_sum, 0)
    pltpu.make_async_copy(sc, sp.at[v], m_rs.at[7]).start()
    for s in range(4):
        lo, hi = (z + 7 - s) % 8, (z + 1 + s) % 8
        if s < 3:
            got(la_part(lo, c), g_rs.at[2 * s])
            got(la_part(hi, c), g_rs.at[2 * s + 1])
            la_step(s + 1, lo, hi)
            la_push(2 * s, hi)
            la_push(2 * s + 1, lo)
        else:
            got(la_part(lo, c, 0, 48), g_rs.at[6])
            got(la_part(lo, c, 48, 32), g_rs.at[7])
            la_push(6, lo)
        if s == 0:
            got(sp, m_rs.at[7])
            s_all = sp[0]
            for n in range(1, 16):
                s_all = s_all + sp[n]
            sz[z] = s_all

            def give_sz(j, _):
                send(sz.at[z], sz.at[z], m_ss.at[8], m_rs.at[8], {"z": (z + j) % 8})
                return 0

            lax.fori_loop(1, 8, give_sz, 0)
    for n in range(7):
        b = zblk(n + 1)
        got(la_part(b, 1 - c), g_rs.at[8 + n])

    def finish(i, _):
        out_ref[i] = other_ref[i] + la[i, pl.ds(0, 75), pl.ds(0, 1200)].astype(F32)
        return 0

    lax.fori_loop(0, 8, finish, 0)
    got(sz.at[pl.ds(0, 7)], m_rs.at[8])
    s_all = sz[0]
    for n in range(1, 8):
        s_all = s_all + sz[n]
    rms_ref[...] = jnp.sqrt(s_all / (8 * 1200 * 1200) + EPS)

    for s in range(4):
        for d in range(2):
            i = 2 * s + d
            if s < 3:
                left(rows(0, 0, 32), r_ss.at[i])
                left(rows(0, 0, 32), r_ss.at[8 + i])
                left(tt.at[0], t_ss.at[i])
                left(la_part(0, 0), g_ss.at[i])
            else:
                left(rows(0, 0, 32), r_ss.at[i])
                left(tt.at[0, pl.ds(0, 48 - 16 * d)], t_ss.at[i])
                left(la_part(0, 0, 0, 48 - 16 * d), g_ss.at[i])
    for n in range(8):
        left(tt.at[0], u_ss.at[n])
    for n in range(7):
        left(la_part(0, 0), g_ss.at[8 + n])
    for n in (0, 1):
        left(rows(0, 0, 16), c_ss.at[n])
        left(xb.at[0, pl.ds(0, 16), pl.ds(0, 256)], c_ss.at[2 + n])
        left(rows(0, 0, 64), c_ss.at[4 + n])
        left(rows(0, 0, 32), c_ss.at[6 + n])
        left(rows(0, 0, 256), c_ss.at[8 + n])
        left(rows(0, 0, 256), c_ss.at[10 + n])
        left(rows(0, 0, 256), c_ss.at[12 + n])
        left(rows(0, 0, 128), c_ss.at[14 + n])

    def drain(k, _):
        for o in (0, 8):
            for n, cnt in ((0, 32), (2, 16), (4, 128), (6, 64)):
                left(rows(0, 0, cnt), x_ss.at[k, o + n])
                left(rows(0, 0, cnt), x_ss.at[k, o + n + 1])
        return 0

    lax.fori_loop(0, 8, drain, 0)

    @pl.when(c == y % 2)
    def _():
        left(zt_ref.at[pl.ds(0, 480)], m_ss.at[0])

    @pl.when(c != y % 2)
    def _():
        left(zt_ref, m_ss.at[0])

    left(hs.at[pl.ds(0, 15)], m_ss.at[1])
    left(hb.at[0], m_ss.at[2])
    left(rb, m_ss.at[3])
    left(bs.at[pl.ds(0, 15)], m_ss.at[4])
    left(ls.at[pl.ds(0, 7)], m_ss.at[5])
    left(lt, m_ss.at[6])
    left(sp.at[pl.ds(0, 15)], m_ss.at[7])
    left(sz.at[pl.ds(0, 7)], m_ss.at[8])


def shards(amplitudes, factors, kernel, other_terms, virt_energy, pair_energy):
    pairs, block, _ = amplitudes.shape
    v = lax.axis_index("x") * 4 + lax.axis_index("y")
    f = jnp.pad(factors, ((0, 5), (0, 0)))
    t = jnp.pad(jnp.transpose(amplitudes, (2, 0, 1)), ((0, 5), (0, 0), (0, 5))).reshape(80, 640)
    zt = kernel.T
    ea = lax.dynamic_slice_in_dim(virt_energy, v * block, block, 0)[:, None]
    eb = virt_energy[None, :]
    vm = pl.BlockSpec(memory_space=pltpu.VMEM)
    V = pltpu.VMEM
    dma = pltpu.SemaphoreType.DMA
    out, rms = pl.pallas_call(
        ladder_kernel,
        out_shape=(
            jax.ShapeDtypeStruct(other_terms.shape, F32),
            jax.ShapeDtypeStruct((8, 128), F32),
        ),
        in_specs=[vm] * 6 + [pl.BlockSpec(memory_space=pltpu.SMEM)],
        out_specs=(vm, vm),
        scratch_shapes=[
            V((8, 1280, 512), BF),
            V((16, 80, 640), BF),
            V((1280, 640), BF),
            V((640, 256), F32),
            V((16, 80, 256), BF),
            V((2, 16, 80, 256), BF),
            V((512, 1280), BF),
            V((8, 2, 32, 512), BF),
            V((512, 512), BF),
            V((512, 1280), F32),
            V((256, 1280), F32),
            V((16, 80, 256), BF),
            V((16, 80, 256), BF),
            V((8, 80, 512), BF),
            V((8, 80, 512), BF),
            V((1280, 128), F32),
            V((1280, 128), F32),
            V((1280, 128), F32),
            V((8, 80, 1280), BF),
            V((8, 128), F32),
            V((16, 8, 128), F32),
            V((8, 8, 128), F32),
            dma((8, 16)), dma((8, 16)),
            dma((16,)), dma((16,)),
            dma((16,)), dma((16,)),
            dma((8,)), dma((8,)),
            dma((8,)), dma((8,)),
            dma((16,)), dma((16,)),
            dma((16,)), dma((16,)),
            dma((4,)),
        ],
        compiler_params=pltpu.CompilerParams(
            collective_id=0, has_side_effects=True, vmem_limit_bytes=60 * 1024 * 1024
        ),
        name="ladder",
    )(f, t, zt, other_terms, ea, eb, pair_energy)
    return out, rms[0, 0]


def solution(mesh):
    torus = Mesh(mesh.devices.reshape(4, 4, 8, 2), ("x", "y", "z", "core"))
    plane, rank = ("x", "y"), ("z", "core")
    return jax.shard_map(
        shards,
        mesh=torus,
        in_specs=(P(None, plane, rank), P(plane, rank), P(plane, rank), P(None, plane, None), P(), P()),
        out_specs=(P(None, plane, None), P()),
        check_vma=False,
    )
```

time: 429 us -> 170 us (0.40)
  waiting for transfers between devices: 163 us -> 0 us
  Pallas kernels: 0 us -> 149 us
  blocking collectives: 112 us -> 0 us
  local copies, waits for them, and re-layouts: 87.1 us -> 19.4 us
  matrix products: 22.5 us -> 0 us
  starting transfers between devices: 18.9 us -> 0 us
  between operations: 16.8 us -> 0.65 us
  other arithmetic: 5.74 us -> 0 us
    pallas_call x0 -> x1, Pallas kernels: none -> 149 us  [shards(): pl.pallas_call(ladder_kernel, out_shape=(jax.ShapeDtypeStruct(other_terms...]
    all_gather x2 -> x0, waiting for transfers between devices: 107 us -> none  [the longest x1 66.2 us: shards(): factor_full = lax.all_gather(factor_rows, VPAIR, axis=0, tiled=True)]
    all_to_all x2 -> x0, blocking collectives: 60.9 us -> none  [the longest x1 43.8 us: sent_to_all(): return lax.all_to_all(copies, axis, split_axis=0, concat_axis=0, tiled=True)]
    all_to_all x3 -> x0, waiting for transfers between devices: 54.8 us -> none  [the longest x1 54.8 us: sent_to_all(): return lax.all_to_all(copies, axis, split_axis=0, concat_axis=0, tiled=True)]
    unnamed x22 -> x4, local copies, waits for them, and re-layouts: 60.5 us -> 13.1 us
    unnamed x1 -> x0, blocking collectives: 33.1 us -> none
    dot_general x3 -> x0, matrix products: 22.5 us -> none  [the longest x1 17.8 us: shards(): jnp.einsum('ap,ipq->iaq', factor_full, weighted, preferred_element_type=j...]
    psum x2 -> x0, blocking collectives: 18.1 us -> none  [one_axis_at_a_time(): shard = lax.psum(shard, axis)]
  transfers between devices with their start and end apart: 6 -> 0, of which waited for: 4 -> 0; matrix products, arithmetic and copies ran while one was open for 14% -> 0% of each run, Pallas kernels for 0% -> 0%
where the time goes in v1:
time: 170 us; the launch traced here: 169 us
  Pallas kernels  149 us (88%)
  local copies, waits for them, and re-layouts  19.4 us (11%)
    pallas_call x1, Pallas kernels, shards(): pl.pallas_call(ladder_kernel, out_shape=(jax.ShapeDtypeStruct(other_terms...  149 us
    unnamed x4, local copies, waits for them, and re-layouts  13.1 us

profile of v1, /device:TPU:1, one launch (start us, length us, event | category | flops | bytes accessed | tf_op | source)
XLA Modules:
  0.0 169.0 jit_solution(13481113627417636352)
XLA Ops:
  0.6 0.8 dynamic-slice_bitcast_fusion
  1.4 1.3 broadcast_in_dim.7.eb_ref
  2.7 0.7 copy.11.ea_ref
  3.4 1.5 pad.8.f_ref
  5.0 1.1 copy.13
  6.1 0.8 reshape.7.t_ref
  6.9 2.0 %copy.9 = bf16[512,512]{0,1:T(8,128)(2,1)} copy(bf16[512,512]{1,0:T(8,128)(2,1)} %param.8) | data formatting | bytes 1048576 | tf_op args[2]
  8.9 4.6 %copy.10.other_ref = f32[8,75,1200]{2,1,0:T(8,128)} copy(f32[8,75,1200]{2,0,1:T(8,128)} %param.9) | data formatting | bytes 5760000 | tf_op args[3]
  13.5 149.0 %ladder.1 = (f32[8,75,1200]{2,1,0:T(8,128)}, f32[8,128]{1,0:T(8,128)}) custom-call(bf16[80,512]{1,0:T(8,128)(2,1)} %pad.8.f_ref, bf16[80,640]{1,0:T(8,128)(2,1)} %reshape.7.t_ref, bf16[512,512]{1,0:T(8,128)(2,1)} %bitcast.5, f32[8,75,1200]{2,1,0:T(8,128)} %copy.10.other_ref, f32[75,1]{1,0:T(8,128)} %copy.11.ea_ref, f32[1,1200]{1,0:T(1,128)} %broadcast_in_dim.7.eb_ref, ...), custom_call_target="tpu_custom_call" | custom-call | tf_op jit(solution)/shard_map/ladder/pallas_call | solution.py:592
  162.5 1.2 slice.3
  163.7 5.3 %copy.12 = f32[8,75,1200]{2,0,1:T(8,128)} copy(f32[8,75,1200]{2,1,0:T(8,128)} %get-tuple-element.6) | data formatting | bytes 5760000
  (1 shorter events, 0.0 us)

commit v2 on v1

--- a/solution.py
+++ b/solution.py
@@ -24,9 +24,10 @@
 
 
 def ladder_kernel(
-    f_ref, t_ref, zt_ref, other_ref, ea_ref, eb_ref, ep_ref, out_ref, rms_ref,
+    f_ref, t_ref, k_ref, other_hbm, e_ref, ep_ref, out_ref, rms_ref,
+    stage, res, zt_ref, er,
     xb, tt, ttp, half, hs, hb, ht, zb_ref, wt, acc, rb, bs, br, ls, lb, lt, ltr, lc, la, sc, sp, sz,
-    x_ss, x_rs, c_ss, c_rs, r_ss, r_rs, t_ss, t_rs, u_ss, u_rs, g_ss, g_rs, m_ss, m_rs, loc,
+    x_ss, x_rs, c_ss, c_rs, r_ss, r_rs, t_ss, t_rs, u_ss, u_rs, g_ss, g_rs, m_ss, m_rs, p_ss, p_rs, q_ss, q_rs, loc,
 ):
     x, y, z, c = (lax.axis_index(n) for n in ("x", "y", "z", "core"))
     v = 4 * x + y
@@ -65,11 +66,12 @@
     own = [
         pltpu.make_async_copy(f_ref.at[pl.ds(0, 32)], rows(z, a_off(x, y), 32), loc.at[0]),
         pltpu.make_async_copy(f_ref.at[pl.ds(32, 32)], rows(z, b_off(x, y), 32), loc.at[1]),
-        pltpu.make_async_copy(f_ref.at[pl.ds(64, 16)], rows(z, c_off(x, y), 16), loc.at[2]),
-        pltpu.make_async_copy(t_ref, tt.at[2 * z + c], loc.at[3]),
     ]
     for o in own:
         o.start()
+
+    others = pltpu.make_async_copy(other_hbm, stage, loc.at[2])
+    others.start()
 
     bar = pltpu.get_barrier_semaphore()
 
@@ -90,9 +92,28 @@
         return 0
 
     lax.fori_loop(1, 8, greet_z, 0)
+    with jax.named_scope("local"):
+        last = jnp.concatenate([f_ref[pl.ds(64, 11), :].astype(F32), jnp.zeros((5, 512), F32)], 0)
+        xb[z, pl.ds(pl.multiple_of(c_off(x, y), 16), 16), :] = last.astype(BF)
+        for n in range(5):
+            cnt = 128 if n < 4 else 88
+            m = t_ref[pl.ds(128 * n, cnt), :].astype(F32)
+            if cnt < 128:
+                m = jnp.concatenate([m, jnp.zeros((128 - cnt, 75), F32)], 0)
+            m = jnp.concatenate([m.T, jnp.zeros((5, 128), F32)], 0)
+            tt[2 * z + c, :, pl.ds(128 * n, 128)] = m.astype(BF)
+        for n in range(4):
+            zt_ref[:, pl.ds(128 * n, 128)] = k_ref[pl.ds(128 * n, 128), :].astype(F32).T.astype(BF)
+        er[:, pl.ds(0, 1200)] = jnp.broadcast_to(e_ref[...], (8, 1200))
+        er[:, pl.ds(1200, 80)] = jnp.zeros((8, 80), F32)
+        others.wait()
+        for n in range(10):
+            w = 128 if n < 9 else 48
+            res[n, :, pl.ds(0, w)] = stage[:, pl.ds(128 * n, w)]
     for o in own:
         o.wait()
-    pl.semaphore_wait(bar, 38)
+    with jax.named_scope('barrier'):
+        pl.semaphore_wait(bar, 38)
 
     def zblk(k):
         return (z + ((k + 1) // 2) * (2 * (k % 2) - 1) + 8) % 8
@@ -279,10 +300,12 @@
 
         def chunk(a, _):
             q = pl.ds(pl.multiple_of(256 * a, 256), 256)
-            half[...] = lax.dot_general(ttp[...], xb[z, :, q], TN, preferred_element_type=F32)
+            m = lax.dot_general(ttp[...], xb[z, :, q], TN, preferred_element_type=F32)
+            half[0] = m[:, :128]
+            half[1] = m[:, 128:]
             for h in range(2):
                 for g in range(2):
-                    part = [half[pl.ds(80 * (4 * g + k), 80), pl.ds(128 * h, 128)] for k in range(4)]
+                    part = [half[h, pl.ds(4 * g + k, 80, stride=8), :] for k in range(4)]
                     for s in range(4):
                         m = roll(part[0], (0 - s) * 32)
                         for k in range(1, 4):
@@ -300,10 +323,12 @@
         pltpu.make_async_copy(hs.at[v], hb.at[c, v], m_rs.at[1]).start()
 
     def take_half():
-        got(hb.at[c], m_rs.at[1])
+        with jax.named_scope('w_hb'):
+            got(hb.at[c], m_rs.at[1])
         send(hb.at[c], hb.at[c], m_ss.at[2], m_rs.at[2], sib)
         acc[...] = jnp.zeros_like(acc)
-        got(hb.at[1 - c], m_rs.at[2])
+        with jax.named_scope('w_hbs'):
+            got(hb.at[1 - c], m_rs.at[2])
         for s in range(2):
             to = pl.ds(256 * s, 256)
             for i in range(4):
@@ -314,7 +339,8 @@
             for i in range(2):
                 m = jnp.concatenate([hb[s, 8 * i + j, pl.ds(64, 16), :] for j in range(8)], 0)
                 ht[to, pl.ds(1024 + 128 * i, 128)] = m.astype(F32).T.astype(BF)
-        got(zb_ref, m_rs.at[0])
+        with jax.named_scope('w_zb'):
+            got(zb_ref, m_rs.at[0])
 
     def compute(k, _):
         b = zblk(k)
@@ -337,7 +363,8 @@
 
                 @pl.when(t == s)
                 def _(s=s):
-                    lo, hi = ring_got(s - 1)
+                    with jax.named_scope('ring_got'):
+                        lo, hi = ring_got(s - 1)
                     if s < 4:
                         ring_step(s, lo, hi)
                         push_t(2 * s - 1, hi)
@@ -347,45 +374,55 @@
 
         @pl.when(t >= 4)
         def _():
-            s5(t - 4)
+            with jax.named_scope('s5'):
+                s5(t - 4)
 
         for s in range(9):
 
             @pl.when(t == s)
             def _(s=s):
-                c_step(s)
+                with jax.named_scope('c_step'):
+                    c_step(s)
 
         @pl.when((t >= 3) & (t < 11))
         def _():
-            s4(t - 3)
+            with jax.named_scope('s4'):
+                s4(t - 3)
 
         @pl.when((t >= 2) & (t < 10))
         def _():
-            s3(t - 2)
+            with jax.named_scope('s3'):
+                s3(t - 2)
 
         @pl.when((t >= 1) & (t < 9))
         def _():
-            s2(t - 1)
+            with jax.named_scope('s2'):
+                s2(t - 1)
 
         @pl.when(t < 8)
         def _():
-            s1(t)
+            with jax.named_scope('s1'):
+                s1(t)
 
         @pl.when(t == 0)
         def _():
-            send_kernel()
+            with jax.named_scope('send_kernel'):
+                send_kernel()
 
         @pl.when(t == 4)
         def _():
-            make_half()
+            with jax.named_scope('make_half'):
+                make_half()
 
         @pl.when(t == READY)
         def _():
-            take_half()
+            with jax.named_scope('take_half'):
+                take_half()
 
         lo = jnp.minimum(jnp.maximum(t - 4, 0), jnp.maximum(2 * (t - READY), 0))
         hi = jnp.minimum(jnp.maximum(t - 3, 0), jnp.maximum(2 * (t - READY + 1), 0))
-        lax.fori_loop(lo, hi, compute, 0)
+        with jax.named_scope('compute'):
+            lax.fori_loop(lo, hi, compute, 0)
         return 0
 
     lax.fori_loop(0, TICKS, tick, 0)
@@ -393,7 +430,8 @@
     mine = pl.ds(pl.multiple_of(256 * c, 256), 256)
     give = acc.at[pl.ds(pl.multiple_of(256 * (1 - c), 256), 256)]
     send(give, rb, m_ss.at[3], m_rs.at[3], sib)
-    got(rb, m_rs.at[3])
+    with jax.named_scope('w_rb'):
+        got(rb, m_rs.at[3])
     for n in range(10):
         a = pl.ds(128 * n, 128)
         m = (acc[mine, a] + rb[:, a]).T.astype(BF)
@@ -407,99 +445,138 @@
             for j in range(8):
                 bs[8 * (n - 8) + j, pl.ds(64, 16), :] = m[16 * j : 16 * j + 16]
 
-    def give_back(j, _):
-        send(bs.at[(v + j) % 16], br.at[v], m_ss.at[4], m_rs.at[4], plane_dev(j, c))
-        return 0
-
-    lax.fori_loop(1, 16, give_back, 0)
-    pltpu.make_async_copy(bs.at[v], br.at[v], m_rs.at[4]).start()
-    got(br, m_rs.at[4])
-
-    lanes = lax.broadcasted_iota(jnp.int32, (80, 128), 1) // 32
-    for g in range(2):
-        for a in range(4):
-            part = [br[4 * a + s, :, pl.ds(128 * g, 128)].astype(F32) for s in range(4)]
-            for k in range(4):
-                m = roll(part[0], (0 - k) * 32)
-                for s in range(1, 4):
-                    m = jnp.where(lanes == s, roll(part[s], (s - k) * 32), m)
-                ls[4 * g + k, :, pl.ds(128 * a, 128)] = m.astype(BF)
-
-    def give_z(j, _):
-        w = (z + j) % 8
-        send(ls.at[w], lb.at[z], m_ss.at[5], m_rs.at[5], {"z": w})
-        return 0
-
-    lax.fori_loop(1, 8, give_z, 0)
-    pltpu.make_async_copy(ls.at[z], lb.at[z], m_rs.at[5]).start()
-    got(lb, m_rs.at[5])
-
-    lt[...] = jnp.zeros_like(lt)
-
-    def lad(b, _):
+    pieces = ((0, 32), (32, 48))
+    for h, (lo, n) in enumerate(pieces):
+
+        def give_back(j, _):
+            w = (v + j) % 16
+            send(bs.at[w, pl.ds(lo, n)], br.at[v, pl.ds(lo, n)], p_ss.at[h], p_rs.at[h], plane_dev(j, c))
+            return 0
+
+        lax.fori_loop(1, 16, give_back, 0)
+        pltpu.make_async_copy(bs.at[v, pl.ds(lo, n)], br.at[v, pl.ds(lo, n)], p_rs.at[h]).start()
+
+    def z_of(j):
+        return (j // 2 + 1) if j % 2 == 0 else 7 - j // 2
+
+    for h, (lo, n) in enumerate(pieces):
+        with jax.named_scope("w_br"):
+            got(br.at[:, pl.ds(lo, n)], p_rs.at[h])
+        with jax.named_scope("unpack"):
+            lanes = lax.broadcasted_iota(jnp.int32, (n, 128), 1) // 32
+            for g in range(2):
+                for a in range(4):
+                    part = [br[4 * a + s, pl.ds(lo, n), pl.ds(128 * g, 128)].astype(F32) for s in range(4)]
+                    for k in range(4):
+                        m = roll(part[0], (0 - k) * 32)
+                        for s in range(1, 4):
+                            m = jnp.where(lanes == s, roll(part[s], (s - k) * 32), m)
+                        ls[4 * g + k, pl.ds(lo, n), pl.ds(128 * a, 128)] = m.astype(BF)
+        for j in range(7):
+            d = z_of(j)
+            w = (z + d) % 8
+            send(ls.at[w, pl.ds(lo, n)], lb.at[z, pl.ds(lo, n)], q_ss.at[h, d], q_rs.at[h, d], {"z": w})
+        if h == 0:
+            lt[...] = jnp.zeros_like(lt)
+
+    def lad(b, src):
         for a in range(5):
             a = pl.ds(256 * a, 256)
-            lt[a, pl.ds(0, 80)] += lax.dot_general(xb[b, a, :], lb[b], NT, preferred_element_type=F32)
+            lt[a, pl.ds(0, 80)] += lax.dot_general(xb[b, a, :], src[b], NT, preferred_element_type=F32)
+
+    lad(z, ls)
+
+    def lad_step(j, _):
+        d = jnp.where(j % 2 == 0, j // 2 + 1, 7 - j // 2)
+        b = (z + 8 - d) % 8
+        with jax.named_scope("w_lb"):
+            for h, (lo, n) in enumerate(pieces):
+                got(lb.at[b, pl.ds(lo, n)], q_rs.at[h, d])
+        with jax.named_scope("w_lad"):
+            lad(b, lb)
         return 0
 
-    lax.fori_loop(0, 8, lad, 0)
+    lax.fori_loop(0, 7, lad_step, 0)
     send(lt, ltr, m_ss.at[6], m_rs.at[6], sib)
-    got(ltr, m_rs.at[6])
+    ea = pltpu.roll(er[...], (1280 - 75 * v) % 1280, 1)[:, :128].T[:75, 0:1]
+    with jax.named_scope("w_ltr"):
+        got(ltr, m_rs.at[6])
     lc[pl.ds(1200, 80), :] = jnp.zeros((80, 128), F32)
     for i in range(4):
         for j in range(4):
             o = 75 * (4 * i + j)
             for n, off, cnt in ((0, a_off(i, j), 32), (32, b_off(i, j), 32), (64, c_off(i, j), 11)):
                 lc[pl.ds(o + n, cnt), :] = lt[pl.ds(off, cnt), :] + ltr[pl.ds(off, cnt), :]
+    for n in range(10):
+        b = pl.ds(128 * n, 128)
+        la[z, :, b] = lc[b, :].T[:80].astype(BF)
+
+    chunks = ((0, 48), (48, 32))
+
+    def la_part(i, h, ch):
+        lo, n = chunks[ch]
+        return la.at[i, pl.ds(lo, n), pl.ds(pl.multiple_of(640 * h, 128), 640)]
+
+    def la_send(s, blk, d, ch):
+        p = la_part(blk, c, ch)
+        send(p, p, g_ss.at[2 * s + d, ch], g_rs.at[2 * s + d, ch], {"z": (zp, zm)[d]})
+
+    def la_push(n, blk, ch):
+        p = la_part(blk, c, ch)
+        send(p, p, g_ss.at[8 + n, ch], g_rs.at[8 + n, ch], sib)
+
+    for ch in range(2):
+        for d in range(2):
+            la_send(0, z, d, ch)
+
     total = jnp.zeros((75, 128), F32)
     ep = ep_ref[z]
     for n in range(10):
-        b = pl.ds(128 * n, 128)
-        m = lc[b, :].T[:80]
-        la[z, :, b] = m.astype(BF)
         w = 128 if n < 9 else 48
         b = pl.ds(128 * n, w)
-        den = ea_ref[...] + eb_ref[:, b] - ep
-        u = (other_ref[z, :, b] + m[:75, :w]) / den
+        den = ea + er[0:1, b] - ep
+        u = (res[n, pl.ds(z, 75, stride=8), :] + lc[pl.ds(128 * n, 128), :].T[:75])[:, :w] / den
         u = u * u
         if w < 128:
             u = jnp.concatenate([u, jnp.zeros((75, 128 - w), F32)], 1)
         total = total + u
     sc[...] = jnp.full((8, 128), jnp.sum(total), F32)
 
-    def la_part(i, h, lo=0, n=80):
-        return la.at[i, pl.ds(lo, n), pl.ds(pl.multiple_of(640 * h, 128), 640)]
-
-    def la_step(s, lo, hi):
-        for d, (blk, dev) in enumerate(((lo, zp), (hi, zm))):
-            p = la_part(blk, c) if s < 3 else la_part(blk, c, 48 * d, 48 - 16 * d)
-            send(p, p, g_ss.at[2 * s + d], g_rs.at[2 * s + d], {"z": dev})
-
-    def la_push(n, blk):
-        send(la_part(blk, c), la_part(blk, c), g_ss.at[8 + n], g_rs.at[8 + n], sib)
-
-    la_step(0, z, z)
-
     def give_sum(j, _):
         send(sc, sp.at[v], m_ss.at[7], m_rs.at[7], plane_dev(j, c))
         return 0
 
     lax.fori_loop(1, 16, give_sum, 0)
     pltpu.make_async_copy(sc, sp.at[v], m_rs.at[7]).start()
+
+    def finish(i):
+        o = pl.ds(i, 75, stride=8)
+        for n in range(10):
+            b = pl.ds(128 * n, 128)
+            res[n, o, :] = res[n, o, :] + la[i, :, b].astype(F32)[:75]
+
     for s in range(4):
         lo, hi = (z + 7 - s) % 8, (z + 1 + s) % 8
-        if s < 3:
-            got(la_part(lo, c), g_rs.at[2 * s])
-            got(la_part(hi, c), g_rs.at[2 * s + 1])
-            la_step(s + 1, lo, hi)
-            la_push(2 * s, hi)
-            la_push(2 * s + 1, lo)
-        else:
-            got(la_part(lo, c, 0, 48), g_rs.at[6])
-            got(la_part(lo, c, 48, 32), g_rs.at[7])
-            la_push(6, lo)
+        with jax.named_scope(f"w_la{s}"):
+            if s < 3:
+                for ch in range(2):
+                    got(la_part(lo, c, ch), g_rs.at[2 * s, ch])
+                    if s < 2 or ch == 0:
+                        la_send(s + 1, lo, 0, ch)
+                    la_push(2 * s + 1, lo, ch)
+                    got(la_part(hi, c, ch), g_rs.at[2 * s + 1, ch])
+                    if s < 2 or ch == 1:
+                        la_send(s + 1, hi, 1, ch)
+                    la_push(2 * s, hi, ch)
+            else:
+                for ch in range(2):
+                    got(la_part(lo, c, ch), g_rs.at[6 + ch, ch])
+                    la_push(6, lo, ch)
         if s == 0:
-            got(sp, m_rs.at[7])
+            finish(z)
+        if s == 1:
+            with jax.named_scope("w_sp"):
+                got(sp, m_rs.at[7])
             s_all = sp[0]
             for n in range(1, 16):
                 s_all = s_all + sp[n]
@@ -510,20 +587,36 @@
                 return 0
 
             lax.fori_loop(1, 8, give_sz, 0)
-    for n in range(7):
-        b = zblk(n + 1)
-        got(la_part(b, 1 - c), g_rs.at[8 + n])
-
-    def finish(i, _):
-        out_ref[i] = other_ref[i] + la[i, pl.ds(0, 75), pl.ds(0, 1200)].astype(F32)
-        return 0
-
-    lax.fori_loop(0, 8, finish, 0)
-    got(sz.at[pl.ds(0, 7)], m_rs.at[8])
+        if s >= 1:
+            for n in (2 * s - 2, 2 * s - 1):
+                with jax.named_scope("w_las"):
+                    for ch in range(2):
+                        got(la_part(zblk(n + 1), 1 - c, ch), g_rs.at[8 + n, ch])
+                with jax.named_scope("finish"):
+                    finish(zblk(n + 1))
+    with jax.named_scope("w_las"):
+        for ch in range(2):
+            got(la_part(zblk(7), 1 - c, ch), g_rs.at[14, ch])
+    with jax.named_scope("finish"):
+        finish(zblk(7))
+    outs = []
+    for lo in range(0, 600, 200):
+        for n in range(10):
+            w = 128 if n < 9 else 48
+            stage[pl.ds(lo, 200), pl.ds(128 * n, w)] = res[n, pl.ds(lo, 200), pl.ds(0, w)]
+        p = pl.ds(lo, 200)
+        outs.append(pltpu.make_async_copy(stage.at[p], out_ref.at[p], loc.at[3 + lo // 200]))
+        outs[-1].start()
+    with jax.named_scope("w_sz"):
+        got(sz.at[pl.ds(0, 7)], m_rs.at[8])
     s_all = sz[0]
     for n in range(1, 8):
         s_all = s_all + sz[n]
-    rms_ref[...] = jnp.sqrt(s_all / (8 * 1200 * 1200) + EPS)
+    s_all = jnp.sqrt(s_all / (8 * 1200 * 1200) + EPS)
+    rms_ref[0, 0] = s_all[0, 0]
+    with jax.named_scope('w_out'):
+        for o in outs:
+            o.wait()
 
     for s in range(4):
         for d in range(2):
@@ -532,15 +625,17 @@
                 left(rows(0, 0, 32), r_ss.at[i])
                 left(rows(0, 0, 32), r_ss.at[8 + i])
                 left(tt.at[0], t_ss.at[i])
-                left(la_part(0, 0), g_ss.at[i])
+                for ch in range(2):
+                    left(la_part(0, 0, ch), g_ss.at[i, ch])
             else:
                 left(rows(0, 0, 32), r_ss.at[i])
                 left(tt.at[0, pl.ds(0, 48 - 16 * d)], t_ss.at[i])
-                left(la_part(0, 0, 0, 48 - 16 * d), g_ss.at[i])
+                left(la_part(0, 0, d), g_ss.at[i, d])
     for n in range(8):
         left(tt.at[0], u_ss.at[n])
     for n in range(7):
-        left(la_part(0, 0), g_ss.at[8 + n])
+        for ch in range(2):
+            left(la_part(0, 0, ch), g_ss.at[8 + n, ch])
     for n in (0, 1):
         left(rows(0, 0, 16), c_ss.at[n])
         left(xb.at[0, pl.ds(0, 16), pl.ds(0, 256)], c_ss.at[2 + n])
@@ -571,37 +666,39 @@
     left(hs.at[pl.ds(0, 15)], m_ss.at[1])
     left(hb.at[0], m_ss.at[2])
     left(rb, m_ss.at[3])
-    left(bs.at[pl.ds(0, 15)], m_ss.at[4])
-    left(ls.at[pl.ds(0, 7)], m_ss.at[5])
+    for h, (lo, n) in enumerate(pieces):
+        left(bs.at[pl.ds(0, 15), pl.ds(lo, n)], p_ss.at[h])
+        for d in range(1, 8):
+            left(ls.at[0, pl.ds(lo, n)], q_ss.at[h, d])
     left(lt, m_ss.at[6])
     left(sp.at[pl.ds(0, 15)], m_ss.at[7])
     left(sz.at[pl.ds(0, 7)], m_ss.at[8])
 
 
 def shards(amplitudes, factors, kernel, other_terms, virt_energy, pair_energy):
-    pairs, block, _ = amplitudes.shape
-    v = lax.axis_index("x") * 4 + lax.axis_index("y")
-    f = jnp.pad(factors, ((0, 5), (0, 0)))
-    t = jnp.pad(jnp.transpose(amplitudes, (2, 0, 1)), ((0, 5), (0, 0), (0, 5))).reshape(80, 640)
-    zt = kernel.T
-    ea = lax.dynamic_slice_in_dim(virt_energy, v * block, block, 0)[:, None]
-    eb = virt_energy[None, :]
+    t = jnp.transpose(amplitudes, (1, 0, 2)).reshape(600, 75)
+    other = jnp.transpose(other_terms, (1, 0, 2)).reshape(600, 1200)
     vm = pl.BlockSpec(memory_space=pltpu.VMEM)
+    sm = pl.BlockSpec(memory_space=pltpu.SMEM)
     V = pltpu.VMEM
     dma = pltpu.SemaphoreType.DMA
     out, rms = pl.pallas_call(
         ladder_kernel,
         out_shape=(
-            jax.ShapeDtypeStruct(other_terms.shape, F32),
-            jax.ShapeDtypeStruct((8, 128), F32),
+            jax.ShapeDtypeStruct((600, 1200), F32),
+            jax.ShapeDtypeStruct((1, 1), F32),
         ),
-        in_specs=[vm] * 6 + [pl.BlockSpec(memory_space=pltpu.SMEM)],
-        out_specs=(vm, vm),
+        in_specs=[vm, vm, vm, pl.BlockSpec(memory_space=pl.ANY), vm, sm],
+        out_specs=(pl.BlockSpec(memory_space=pl.ANY), sm),
         scratch_shapes=[
+            V((600, 1200), F32),
+            V((10, 600, 128), F32),
+            V((512, 512), BF),
+            V((8, 1280), F32),
             V((8, 1280, 512), BF),
             V((16, 80, 640), BF),
             V((1280, 640), BF),
-            V((640, 256), F32),
+            V((2, 640, 128), F32),
             V((16, 80, 256), BF),
             V((2, 16, 80, 256), BF),
             V((512, 1280), BF),
@@ -625,16 +722,18 @@
             dma((16,)), dma((16,)),
             dma((8,)), dma((8,)),
             dma((8,)), dma((8,)),
+            dma((16, 2)), dma((16, 2)),
             dma((16,)), dma((16,)),
-            dma((16,)), dma((16,)),
-            dma((4,)),
+            dma((2,)), dma((2,)),
+            dma((2, 8)), dma((2, 8)),
+            dma((12,)),
         ],
         compiler_params=pltpu.CompilerParams(
             collective_id=0, has_side_effects=True, vmem_limit_bytes=60 * 1024 * 1024
         ),
         name="ladder",
-    )(f, t, zt, other_terms, ea, eb, pair_energy)
-    return out, rms[0, 0]
+    )(factors, t, kernel, other, virt_energy[None, :], pair_energy)
+    return jnp.transpose(out.reshape(75, 8, 1200), (1, 0, 2)), rms.reshape(())
 
 
 def solution(mesh):

time: 170 us -> 147 us (0.86)
  local copies, waits for them, and re-layouts: 19.4 us -> 5 us
  Pallas kernels: 149 us -> 140 us
  between operations: 0.65 us -> 2.44 us
    unnamed x4 -> x1, local copies, waits for them, and re-layouts: 13.1 us -> 3.71 us
    pallas_call x1, Pallas kernels: 149 us -> 140 us  [shards(): pl.pallas_call(ladder_kernel, out_shape=(jax.ShapeDtypeStruct((600, 1200)...]
where the time goes in v2:
time: 147 us
  Pallas kernels  140 us (95%)
  local copies, waits for them, and re-layouts  5 us (3%)
  between operations  2.44 us (2%)
    pallas_call x1, Pallas kernels, shards(): pl.pallas_call(ladder_kernel, out_shape=(jax.ShapeDtypeStruct((600, 1200)...  140 us
    unnamed x1, local copies, waits for them, and re-layouts  3.71 us

profile of v2, /device:TPU:1, one launch (start us, length us, event | category | flops | bytes accessed | tf_op | source)
XLA Modules:
  0.0 147.2 jit_solution(2841450631210916668)
XLA Ops:
  0.6 1.3 broadcast_in_dim.3.e_ref
  1.9 139.8 %ladder.1 = (f32[600,1200]{1,0:T(8,128)}, f32[1,1]{1,0:T(1,128)}) custom-call(bf16[75,512]{1,0:T(8,128)(2,1)} %f_ref.1, bf16[600,75]{1,0:T(8,128)(2,1)} %bitcast.12, bf16[512,512]{1,0:T(8,128)(2,1)} %k_ref.1, f32[600,1200]{1,0:T(8,128)} %bitcast.10, f32[1,1200]{1,0:T(1,128)} %broadcast_in_dim.3.e_ref, f32[8]{0:T(128)} %ep_ref.1), custom_call_target="tpu_custom_call" | custom-call | tf_op jit(solution)/shard_map/ladder/pallas_call | solution.py:685
  141.7 3.7 %copy.10 = f32[8,75,1200]{2,0,1:T(8,128)} copy(f32[8,75,1200]{2,0,1:T(8,128)} %bitcast.11) | data formatting | bytes 5760000

commit v3 on v2

--- a/solution.py
+++ b/solution.py
@@ -16,6 +16,7 @@
 TN = (((0,), (0,)), ((), ()))
 TICKS = 12
 READY = 6
+FAR = sorted(((i, j) for i in range(4) for j in range(4) if i or j), key=lambda p: -min(p[0], 4 - p[0]) - min(p[1], 4 - p[1]))
 
 
 def roll(a, shift):
@@ -36,8 +37,8 @@
     zp, zm = (z + 1) % 8, (z + 7) % 8
     sib = {"core": 1 - c}
 
-    def rows(i, off, n, ref=None):
-        return (xb if ref is None else ref).at[i, pl.ds(pl.multiple_of(off, 16), n)]
+    def rows(i, off, n, w=512, lo=0):
+        return xb.at[i, pl.ds(pl.multiple_of(off, 16), n), pl.ds(lo, w)]
 
     def send(src, dst, ss, rs, dev):
         pltpu.make_async_remote_copy(
@@ -118,23 +119,23 @@
     def zblk(k):
         return (z + ((k + 1) // 2) * (2 * (k % 2) - 1) + 8) % 8
 
+    def ring_pieces(s, d, blk):
+        a, b = rows(blk, a_off(x, y), 32, 384), rows(blk, b_off(x, y), 32, 384)
+        return ((a, 2 * s + d), (b, 8 + 2 * s + d)) if s < 3 else (((a, b)[d], 6 + d),)
+
+    def t_piece(s, d, blk):
+        r = 2 * blk + c
+        return tt.at[r] if s < 3 else tt.at[r, pl.ds(48 * d, 48 - 16 * d)]
+
     def ring_step(s, zl, zr):
-        for d, (blk, dev) in enumerate(((zl, zp), (zr, zm))):
-            i = 2 * s + d
-            dev = {"z": dev}
-            r = 2 * blk + c
-            if s < 3:
-                for o in (a_off(x, y), b_off(x, y)):
-                    w = 0 if o is None else o
-                send(rows(blk, a_off(x, y), 32), rows(blk, a_off(x, y), 32), r_ss.at[i], r_rs.at[i], dev)
-                send(rows(blk, b_off(x, y), 32), rows(blk, b_off(x, y), 32), r_ss.at[8 + i], r_rs.at[8 + i], dev)
-                send(tt.at[r], tt.at[r], t_ss.at[i], t_rs.at[i], dev)
-            elif d == 0:
-                send(rows(blk, a_off(x, y), 32), rows(blk, a_off(x, y), 32), r_ss.at[i], r_rs.at[i], dev)
-                send(tt.at[r, pl.ds(0, 48)], tt.at[r, pl.ds(0, 48)], t_ss.at[i], t_rs.at[i], dev)
-            else:
-                send(rows(blk, b_off(x, y), 32), rows(blk, b_off(x, y), 32), r_ss.at[i], r_rs.at[i], dev)
-                send(tt.at[r, pl.ds(48, 32)], tt.at[r, pl.ds(48, 32)], t_ss.at[i], t_rs.at[i], dev)
+        for d, blk in enumerate((zl, zr)):
+            for p, i in ring_pieces(s, d, blk):
+                send(p, p, r_ss.at[i], r_rs.at[i], {"z": (zp, zm)[d]})
+
+    def t_step(s, zl, zr):
+        for d, blk in enumerate((zl, zr)):
+            p = t_piece(s, d, blk)
+            send(p, p, t_ss.at[2 * s + d], t_rs.at[2 * s + d], {"z": (zp, zm)[d]})
 
     def push_t(n, blk):
         r = 2 * blk + c
@@ -143,21 +144,18 @@
     def ring_got(s):
         lo, hi = (z + 7 - s) % 8, (z + 1 + s) % 8
         for d, blk in enumerate((lo, hi)):
-            i = 2 * s + d
-            r = 2 * blk + c
-            if s < 3:
-                got(rows(blk, a_off(x, y), 32), r_rs.at[i])
-                got(rows(blk, b_off(x, y), 32), r_rs.at[8 + i])
-                got(tt.at[r], t_rs.at[i])
-            elif d == 0:
-                got(rows(blk, a_off(x, y), 32), r_rs.at[i])
-                got(tt.at[r, pl.ds(0, 48)], t_rs.at[i])
-            else:
-                got(rows(blk, b_off(x, y), 32), r_rs.at[i])
-                got(tt.at[r, pl.ds(48, 32)], t_rs.at[i])
+            for p, i in ring_pieces(s, d, blk):
+                got(p, r_rs.at[i])
         return lo, hi
 
+    def t_got(s):
+        lo, hi = (z + 7 - s) % 8, (z + 1 + s) % 8
+        for d, blk in enumerate((lo, hi)):
+            got(t_piece(s, d, blk), t_rs.at[2 * s + d])
+        return lo, hi
+
     ring_step(0, z, z)
+    t_step(0, z, z)
     push_t(0, z)
 
     def c_piece(i, j, h):
@@ -187,83 +185,82 @@
             send(p, p, c_ss.at[6], c_rs.at[6], {"x": xp})
             send(q, q, c_ss.at[7], c_rs.at[7], {"x": xm})
         else:
+            g = s - 5
             if s == 4:
                 got(rows(z, c_off((x + 2) % 4, 0), 32), c_rs.at[6])
                 got(rows(z, c_off((x + 2) % 4, 2), 32), c_rs.at[7])
             else:
-                g = s - 5
-                lo, hi = (z + 7 - g) % 8, (z + 1 + g) % 8
-                i = 8 + 2 * g
-                if g < 3:
-                    got(rows(lo, 1024, 256), c_rs.at[i])
-                    got(rows(hi, 1024, 256), c_rs.at[i + 1])
-                else:
-                    got(rows(lo, 1024, 128), c_rs.at[i])
-                    got(rows(hi, 1152, 128), c_rs.at[i + 1])
+                for d, blk in enumerate(((z + 7 - g) % 8, (z + 1 + g) % 8)):
+                    for p, i in c_ring(g, d, blk):
+                        got(p, c_rs.at[i])
             if s < 8:
-                h = s - 4
-                i = 8 + 2 * h
-                lo, hi = (z + 8 - h) % 8, (z + h) % 8
-                n = 256 if h < 3 else 128
-                o = 1024 if h < 3 else 1152
-                send(rows(lo, 1024, n), rows(lo, 1024, n), c_ss.at[i], c_rs.at[i], {"z": zp})
-                send(rows(hi, o, n), rows(hi, o, n), c_ss.at[i + 1], c_rs.at[i + 1], {"z": zm})
-
-    def s1(k):
+                g += 1
+                for d, blk in enumerate(((z + 8 - g) % 8, (z + g) % 8)):
+                    for p, i in c_ring(g, d, blk):
+                        send(p, p, c_ss.at[i], c_rs.at[i], {"z": (zp, zm)[d]})
+
+    def c_ring(g, d, blk):
+        n = 1 if g < 3 else 2
+        return (
+            (rows(blk, 1024 + (0 if n == 1 else 128 * d), 256 // n), 8 + 2 * g + d),
+            (rows(blk, 0 if n == 1 else 512 * d, 1024 // n, 128, 384), 16 + 2 * g + d),
+        )
+
+    def s1(k, w=384):
         b = zblk(k)
-        p, q = rows(b, a_off(x, y), 32), rows(b, b_off(x, y), 32)
+        p, q = rows(b, a_off(x, y), 32, w), rows(b, b_off(x, y), 32, w)
         send(p, p, x_ss.at[k, 0], x_rs.at[k, 0], {"y": yp})
         send(p, p, x_ss.at[k, 1], x_rs.at[k, 1], {"y": ym})
         send(q, q, x_ss.at[k, 8], x_rs.at[k, 8], {"x": xp})
         send(q, q, x_ss.at[k, 9], x_rs.at[k, 9], {"x": xm})
 
-    def s2(k):
+    def s2(k, w=384):
         b = zblk(k)
-        got(rows(b, a_off(x, ym), 32), x_rs.at[k, 0])
-        got(rows(b, a_off(x, yp), 32), x_rs.at[k, 1])
-        p, q = rows(b, a_off(x, ym), 16), rows(b, a_off(x, yp) + 16, 16)
+        got(rows(b, a_off(x, ym), 32, w), x_rs.at[k, 0])
+        got(rows(b, a_off(x, yp), 32, w), x_rs.at[k, 1])
+        p, q = rows(b, a_off(x, ym), 16, w), rows(b, a_off(x, yp) + 16, 16, w)
         send(p, p, x_ss.at[k, 2], x_rs.at[k, 2], {"y": yp})
         send(q, q, x_ss.at[k, 3], x_rs.at[k, 3], {"y": ym})
-        got(rows(b, b_off(xm, y), 32), x_rs.at[k, 8])
-        got(rows(b, b_off(xp, y), 32), x_rs.at[k, 9])
-        p, q = rows(b, b_off(xm, y), 16), rows(b, b_off(xp, y) + 16, 16)
+        got(rows(b, b_off(xm, y), 32, w), x_rs.at[k, 8])
+        got(rows(b, b_off(xp, y), 32, w), x_rs.at[k, 9])
+        p, q = rows(b, b_off(xm, y), 16, w), rows(b, b_off(xp, y) + 16, 16, w)
         send(p, p, x_ss.at[k, 10], x_rs.at[k, 10], {"x": xp})
         send(q, q, x_ss.at[k, 11], x_rs.at[k, 11], {"x": xm})
 
-    def s3(k):
+    def s3(k, w=384):
         b = zblk(k)
         y2, x2 = (y + 2) % 4, (x + 2) % 4
-        got(rows(b, a_off(x, y2), 16), x_rs.at[k, 2])
-        got(rows(b, a_off(x, y2) + 16, 16), x_rs.at[k, 3])
-        p = rows(b, a_off(x, 0), 128)
+        got(rows(b, a_off(x, y2), 16, w), x_rs.at[k, 2])
+        got(rows(b, a_off(x, y2) + 16, 16, w), x_rs.at[k, 3])
+        p = rows(b, a_off(x, 0), 128, w)
         send(p, p, x_ss.at[k, 4], x_rs.at[k, 4], {"x": xp})
         send(p, p, x_ss.at[k, 5], x_rs.at[k, 5], {"x": xm})
-        got(rows(b, b_off(x2, y), 16), x_rs.at[k, 10])
-        got(rows(b, b_off(x2, y) + 16, 16), x_rs.at[k, 11])
-        p = rows(b, b_off(0, y), 128)
+        got(rows(b, b_off(x2, y), 16, w), x_rs.at[k, 10])
+        got(rows(b, b_off(x2, y) + 16, 16, w), x_rs.at[k, 11])
+        p = rows(b, b_off(0, y), 128, w)
         send(p, p, x_ss.at[k, 12], x_rs.at[k, 12], {"y": yp})
         send(p, p, x_ss.at[k, 13], x_rs.at[k, 13], {"y": ym})
 
-    def s4(k):
+    def s4(k, w=384):
         b = zblk(k)
-        got(rows(b, a_off(xm, 0), 128), x_rs.at[k, 4])
-        got(rows(b, a_off(xp, 0), 128), x_rs.at[k, 5])
-        p, q = rows(b, a_off(xm, 0), 64), rows(b, a_off(xp, 2), 64)
+        got(rows(b, a_off(xm, 0), 128, w), x_rs.at[k, 4])
+        got(rows(b, a_off(xp, 0), 128, w), x_rs.at[k, 5])
+        p, q = rows(b, a_off(xm, 0), 64, w), rows(b, a_off(xp, 2), 64, w)
         send(p, p, x_ss.at[k, 6], x_rs.at[k, 6], {"x": xp})
         send(q, q, x_ss.at[k, 7], x_rs.at[k, 7], {"x": xm})
-        got(rows(b, b_off(0, ym), 128), x_rs.at[k, 12])
-        got(rows(b, b_off(0, yp), 128), x_rs.at[k, 13])
-        p, q = rows(b, b_off(0, ym), 64), rows(b, b_off(2, yp), 64)
+        got(rows(b, b_off(0, ym), 128, w), x_rs.at[k, 12])
+        got(rows(b, b_off(0, yp), 128, w), x_rs.at[k, 13])
+        p, q = rows(b, b_off(0, ym), 64, w), rows(b, b_off(2, yp), 64, w)
         send(p, p, x_ss.at[k, 14], x_rs.at[k, 14], {"y": yp})
         send(q, q, x_ss.at[k, 15], x_rs.at[k, 15], {"y": ym})
 
-    def s5(k):
+    def s5(k, w=384):
         b = zblk(k)
         y2, x2 = (y + 2) % 4, (x + 2) % 4
-        got(rows(b, a_off(x2, 0), 64), x_rs.at[k, 6])
-        got(rows(b, a_off(x2, 2), 64), x_rs.at[k, 7])
-        got(rows(b, b_off(0, y2), 64), x_rs.at[k, 14])
-        got(rows(b, b_off(2, y2), 64), x_rs.at[k, 15])
+        got(rows(b, a_off(x2, 0), 64, w), x_rs.at[k, 6])
+        got(rows(b, a_off(x2, 2), 64, w), x_rs.at[k, 7])
+        got(rows(b, b_off(0, y2), 64, w), x_rs.at[k, 14])
+        got(rows(b, b_off(2, y2), 64, w), x_rs.at[k, 15])
 
     def send_kernel():
         kc = y % 2
@@ -357,75 +354,59 @@
             acc[:, a] += lax.dot_general(wt[...], xb[b, a, :], NT, preferred_element_type=F32)
         return 0
 
+    def on(cond, name, f, *args):
+        @pl.when(cond)
+        def _():
+            with jax.named_scope(name):
+                f(*args)
+
+    def forward(s):
+        lo, hi = ring_got(s - 1)
+        if s < 4:
+            ring_step(s, lo, hi)
+
+    def forward_t(s):
+        lo, hi = t_got(s - 1)
+        if s < 4:
+            t_step(s, lo, hi)
+            push_t(2 * s - 1, hi)
+            push_t(2 * s, lo)
+        else:
+            push_t(7, lo)
+
     def tick(t, _):
-        for s in range(1, 9):
-            if s <= 4:
-
-                @pl.when(t == s)
-                def _(s=s):
-                    with jax.named_scope('ring_got'):
-                        lo, hi = ring_got(s - 1)
-                    if s < 4:
-                        ring_step(s, lo, hi)
-                        push_t(2 * s - 1, hi)
-                        push_t(2 * s, lo)
-                    else:
-                        push_t(7, lo)
-
-        @pl.when(t >= 4)
-        def _():
-            with jax.named_scope('s5'):
-                s5(t - 4)
-
-        for s in range(9):
-
-            @pl.when(t == s)
-            def _(s=s):
-                with jax.named_scope('c_step'):
-                    c_step(s)
-
-        @pl.when((t >= 3) & (t < 11))
-        def _():
-            with jax.named_scope('s4'):
-                s4(t - 3)
-
-        @pl.when((t >= 2) & (t < 10))
-        def _():
-            with jax.named_scope('s3'):
-                s3(t - 2)
-
-        @pl.when((t >= 1) & (t < 9))
-        def _():
-            with jax.named_scope('s2'):
-                s2(t - 1)
-
-        @pl.when(t < 8)
-        def _():
-            with jax.named_scope('s1'):
-                s1(t)
-
-        @pl.when(t == 0)
-        def _():
-            with jax.named_scope('send_kernel'):
-                send_kernel()
-
-        @pl.when(t == 4)
-        def _():
-            with jax.named_scope('make_half'):
-                make_half()
-
-        @pl.when(t == READY)
-        def _():
-            with jax.named_scope('take_half'):
-                take_half()
-
-        lo = jnp.minimum(jnp.maximum(t - 4, 0), jnp.maximum(2 * (t - READY), 0))
-        hi = jnp.minimum(jnp.maximum(t - 3, 0), jnp.maximum(2 * (t - READY + 1), 0))
-        with jax.named_scope('compute'):
+        for s in range(1, 5):
+            on(t == s, "forward", forward, s)
+        on(t == 4, "s5", s5, 0, 512)
+        on(t > 4, "s5", s5, t - 4)
+        for s in range(5):
+            on(t == s, "c_step", c_step, s)
+        on(t == 3, "s4", s4, 0, 512)
+        on((t > 3) & (t < 11), "s4", s4, t - 3)
+        on(t == 2, "s3", s3, 0, 512)
+        on((t > 2) & (t < 10), "s3", s3, t - 2)
+        on(t == 1, "s2", s2, 0, 512)
+        on((t > 1) & (t < 9), "s2", s2, t - 1)
+        on(t == 0, "s1", s1, 0, 512)
+        on((t > 0) & (t < 8), "s1", s1, t)
+        on(t == 0, "send_kernel", send_kernel)
+        for s in range(1, 5):
+            on(t == s, "forward_t", forward_t, s)
+        on(t == 4, "make_half", make_half)
+        for s in range(5, 8):
+            on(t == 2 * s - 4, "c_step", c_step, s)
+        on(t == READY, "take_half", take_half)
+        with jax.named_scope("compute"):
+            lo = jnp.maximum(t - READY, 0)
+            hi = jnp.maximum(t - READY + 1, 0) + (t >= 11).astype(jnp.int32)
             lax.fori_loop(lo, hi, compute, 0)
         return 0
 
     lax.fori_loop(0, TICKS, tick, 0)
+    with jax.named_scope('c_step'):
+        c_step(8)
+    with jax.named_scope('compute'):
+        compute(7, 0)
 
     mine = pl.ds(pl.multiple_of(256 * c, 256), 256)
     give = acc.at[pl.ds(pl.multiple_of(256 * (1 - c), 256), 256)]
@@ -448,16 +429,11 @@
     pieces = ((0, 32), (32, 48))
     for h, (lo, n) in enumerate(pieces):
 
-        def give_back(j, _):
-            w = (v + j) % 16
-            send(bs.at[w, pl.ds(lo, n)], br.at[v, pl.ds(lo, n)], p_ss.at[h], p_rs.at[h], plane_dev(j, c))
-            return 0
-
-        lax.fori_loop(1, 16, give_back, 0)
+        for i, j in FAR:
+            i, j = (x + i) % 4, (y + j) % 4
+            w = 4 * i + j
+            send(bs.at[w, pl.ds(lo, n)], br.at[v, pl.ds(lo, n)], p_ss.at[h], p_rs.at[h], {"x": i, "y": j})
         pltpu.make_async_copy(bs.at[v, pl.ds(lo, n)], br.at[v, pl.ds(lo, n)], p_rs.at[h]).start()
-
-    def z_of(j):
-        return (j // 2 + 1) if j % 2 == 0 else 7 - j // 2
 
     for h, (lo, n) in enumerate(pieces):
         with jax.named_scope("w_br"):
@@ -472,8 +448,7 @@
                         for s in range(1, 4):
                             m = jnp.where(lanes == s, roll(part[s], (s - k) * 32), m)
                         ls[4 * g + k, pl.ds(lo, n), pl.ds(128 * a, 128)] = m.astype(BF)
-        for j in range(7):
-            d = z_of(j)
+        for d in (4, 3, 5, 2, 6, 1, 7):
             w = (z + d) % 8
             send(ls.at[w, pl.ds(lo, n)], lb.at[z, pl.ds(lo, n)], q_ss.at[h, d], q_rs.at[h, d], {"z": w})
         if h == 0:
@@ -487,7 +462,7 @@
     lad(z, ls)
 
     def lad_step(j, _):
-        d = jnp.where(j % 2 == 0, j // 2 + 1, 7 - j // 2)
+        d = 4 + ((j + 1) // 2) * (1 - 2 * (j % 2))
         b = (z + 8 - d) % 8
         with jax.named_scope("w_lb"):
             for h, (lo, n) in enumerate(pieces):
@@ -622,13 +597,13 @@
         for d in range(2):
             i = 2 * s + d
             if s < 3:
-                left(rows(0, 0, 32), r_ss.at[i])
-                left(rows(0, 0, 32), r_ss.at[8 + i])
+                left(rows(0, 0, 32, 384), r_ss.at[i])
+                left(rows(0, 0, 32, 384), r_ss.at[8 + i])
                 left(tt.at[0], t_ss.at[i])
                 for ch in range(2):
                     left(la_part(0, 0, ch), g_ss.at[i, ch])
             else:
-                left(rows(0, 0, 32), r_ss.at[i])
+                left(rows(0, 0, 32, 384), r_ss.at[i])
                 left(tt.at[0, pl.ds(0, 48 - 16 * d)], t_ss.at[i])
                 left(la_part(0, 0, d), g_ss.at[i, d])
     for n in range(8):
@@ -641,19 +616,19 @@
         left(xb.at[0, pl.ds(0, 16), pl.ds(0, 256)], c_ss.at[2 + n])
         left(rows(0, 0, 64), c_ss.at[4 + n])
         left(rows(0, 0, 32), c_ss.at[6 + n])
-        left(rows(0, 0, 256), c_ss.at[8 + n])
-        left(rows(0, 0, 256), c_ss.at[10 + n])
-        left(rows(0, 0, 256), c_ss.at[12 + n])
-        left(rows(0, 0, 128), c_ss.at[14 + n])
-
-    def drain(k, _):
+        for g in range(4):
+            for p, i in c_ring(g, n, 0):
+                left(p, c_ss.at[i])
+
+    def drain(k, w):
         for o in (0, 8):
             for n, cnt in ((0, 32), (2, 16), (4, 128), (6, 64)):
-                left(rows(0, 0, cnt), x_ss.at[k, o + n])
-                left(rows(0, 0, cnt), x_ss.at[k, o + n + 1])
-        return 0
-
-    lax.fori_loop(0, 8, drain, 0)
+                left(rows(0, 0, cnt, w), x_ss.at[k, o + n])
+                left(rows(0, 0, cnt, w), x_ss.at[k, o + n + 1])
+        return w
+
+    drain(0, 512)
+    lax.fori_loop(1, 8, lambda k, _: drain(k, 384) * 0, 0)
 
     @pl.when(c == y % 2)
     def _():
@@ -718,7 +693,7 @@
             V((16, 8, 128), F32),
             V((8, 8, 128), F32),
             dma((8, 16)), dma((8, 16)),
-            dma((16,)), dma((16,)),
+            dma((24,)), dma((24,)),
             dma((16,)), dma((16,)),
             dma((8,)), dma((8,)),
             dma((8,)), dma((8,)),

time: 147 us -> 149 us (1.014)
  Pallas kernels: 140 us -> 142 us
    pallas_call x1, Pallas kernels: 140 us -> 142 us  [shards(): pl.pallas_call(ladder_kernel, out_shape=(jax.ShapeDtypeStruct((600, 1200)...]
where the time goes in v3:
time: 149 us
  Pallas kernels  142 us (95%)
  local copies, waits for them, and re-layouts  5 us (3%)
  between operations  2.44 us (2%)
    pallas_call x1, Pallas kernels, shards(): pl.pallas_call(ladder_kernel, out_shape=(jax.ShapeDtypeStruct((600, 1200)...  142 us
    unnamed x1, local copies, waits for them, and re-layouts  3.71 us

profile of v3, /device:TPU:1, one launch (start us, length us, event | category | flops | bytes accessed | tf_op | source)
XLA Modules:
  0.0 149.0 jit_solution(2706159672063562439)
XLA Ops:
  0.6 1.3 broadcast_in_dim.3.e_ref
  1.9 141.5 %ladder.1 = (f32[600,1200]{1,0:T(8,128)}, f32[1,1]{1,0:T(1,128)}) custom-call(bf16[75,512]{1,0:T(8,128)(2,1)} %f_ref.1, bf16[600,75]{1,0:T(8,128)(2,1)} %bitcast.12, bf16[512,512]{1,0:T(8,128)(2,1)} %k_ref.1, f32[600,1200]{1,0:T(8,128)} %bitcast.10, f32[1,1200]{1,0:T(1,128)} %broadcast_in_dim.3.e_ref, f32[8]{0:T(128)} %ep_ref.1), custom_call_target="tpu_custom_call" | custom-call | tf_op jit(solution)/shard_map/ladder/pallas_call | solution.py:660
  143.4 3.7 %copy.10 = f32[8,75,1200]{2,0,1:T(8,128)} copy(f32[8,75,1200]{2,0,1:T(8,128)} %bitcast.11) | data formatting | bytes 5760000

commit v4 on v3

--- a/solution.py
+++ b/solution.py
@@ -14,7 +14,7 @@
 EPS = 1e-06
 NT = (((1,), (1,)), ((), ()))
 TN = (((0,), (0,)), ((), ()))
-TICKS = 12
+TICKS = 14
 READY = 6
 FAR = sorted(((i, j) for i in range(4) for j in range(4) if i or j), key=lambda p: -min(p[0], 4 - p[0]) - min(p[1], 4 - p[1]))
 
@@ -28,7 +28,7 @@
     f_ref, t_ref, k_ref, other_hbm, e_ref, ep_ref, out_ref, rms_ref,
     stage, res, zt_ref, er,
     xb, tt, ttp, half, hs, hb, ht, zb_ref, wt, acc, rb, bs, br, ls, lb, lt, ltr, lc, la, sc, sp, sz,
-    x_ss, x_rs, c_ss, c_rs, r_ss, r_rs, t_ss, t_rs, u_ss, u_rs, g_ss, g_rs, m_ss, m_rs, p_ss, p_rs, q_ss, q_rs, loc,
+    x_ss, x_rs, e_ss, e_rs, c_ss, c_rs, r_ss, r_rs, t_ss, t_rs, u_ss, u_rs, g_ss, g_rs, m_ss, m_rs, p_ss, p_rs, q_ss, q_rs, loc,
 ):
     x, y, z, c = (lax.axis_index(n) for n in ("x", "y", "z", "core"))
     v = 4 * x + y
@@ -120,8 +120,9 @@
         return (z + ((k + 1) // 2) * (2 * (k % 2) - 1) + 8) % 8
 
     def ring_pieces(s, d, blk):
-        a, b = rows(blk, a_off(x, y), 32, 384), rows(blk, b_off(x, y), 32, 384)
-        return ((a, 2 * s + d), (b, 8 + 2 * s + d)) if s < 3 else (((a, b)[d], 6 + d),)
+        a = rows(blk, a_off(x, y), 32, 512 if d or s == 3 else 384)
+        b = rows(blk, b_off(x, y), 32, 384 if d and s < 3 else 512)
+        return ((a, 2 * s + d), (b, 8 + 2 * s + d)) if s < 3 else (((b, a)[d], 6 + d),)
 
     def t_piece(s, d, blk):
         r = 2 * blk + c
@@ -185,82 +186,103 @@
             send(p, p, c_ss.at[6], c_rs.at[6], {"x": xp})
             send(q, q, c_ss.at[7], c_rs.at[7], {"x": xm})
         else:
-            g = s - 5
-            if s == 4:
-                got(rows(z, c_off((x + 2) % 4, 0), 32), c_rs.at[6])
-                got(rows(z, c_off((x + 2) % 4, 2), 32), c_rs.at[7])
-            else:
-                for d, blk in enumerate(((z + 7 - g) % 8, (z + 1 + g) % 8)):
-                    for p, i in c_ring(g, d, blk):
-                        got(p, c_rs.at[i])
-            if s < 8:
-                g += 1
-                for d, blk in enumerate(((z + 8 - g) % 8, (z + g) % 8)):
-                    for p, i in c_ring(g, d, blk):
-                        send(p, p, c_ss.at[i], c_rs.at[i], {"z": (zp, zm)[d]})
-
-    def c_ring(g, d, blk):
-        n = 1 if g < 3 else 2
-        return (
-            (rows(blk, 1024 + (0 if n == 1 else 128 * d), 256 // n), 8 + 2 * g + d),
-            (rows(blk, 0 if n == 1 else 512 * d, 1024 // n, 128, 384), 16 + 2 * g + d),
-        )
-
-    def s1(k, w=384):
+            got(rows(z, c_off((x + 2) % 4, 0), 32), c_rs.at[6])
+            got(rows(z, c_off((x + 2) % 4, 2), 32), c_rs.at[7])
+
+    def quarter(blk, q, d, half_only):
+        xq, yq = (x + q) % 4, (y + q) % 4
+        a, b = rows(blk, xq * 128, 128, 128, 384), rows(blk, 512 + yq * 128, 128, 128, 384)
+        if half_only:
+            return (rows(blk, 1024 + xq * 64 + 32 * d, 32),)
+        return (a, b)[d], rows(blk, 1024 + xq * 64, 64)
+
+    def quarter_send(g, q, blks, half_only=False):
+        for d, blk in enumerate(blks):
+            for p in quarter(blk, q, d, half_only):
+                send(p, p, e_ss.at[g, q, d], e_rs.at[g, q, d], {"z": (zp, zm)[d]})
+
+    def pump(e, _):
+        g, i = e // 4, e % 4
+        q = i + (i == 2).astype(jnp.int32) - (i == 3).astype(jnp.int32)
+        blks = (z + 7 - g) % 8, (z + 1 + g) % 8
+
+        def take(n):
+            for d in range(2):
+                got(rows(blks[d], 0, n), e_rs.at[g, q, d])
+
+        @pl.when(g < 3)
+        def _():
+            take(96)
+
+        @pl.when(g == 3)
+        def _():
+            take(32)
+
+        @pl.when(g < 2)
+        def _():
+            quarter_send(g + 1, q, blks)
+
+        @pl.when(g == 2)
+        def _():
+            quarter_send(g + 1, q, blks, True)
+
+        return 0
+
+    def s1(k, wa, wb):
         b = zblk(k)
-        p, q = rows(b, a_off(x, y), 32, w), rows(b, b_off(x, y), 32, w)
+        p, q = rows(b, a_off(x, y), 32, wa), rows(b, b_off(x, y), 32, wb)
         send(p, p, x_ss.at[k, 0], x_rs.at[k, 0], {"y": yp})
         send(p, p, x_ss.at[k, 1], x_rs.at[k, 1], {"y": ym})
         send(q, q, x_ss.at[k, 8], x_rs.at[k, 8], {"x": xp})
         send(q, q, x_ss.at[k, 9], x_rs.at[k, 9], {"x": xm})
 
-    def s2(k, w=384):
+    def s2(k, wa, wb):
         b = zblk(k)
-        got(rows(b, a_off(x, ym), 32, w), x_rs.at[k, 0])
-        got(rows(b, a_off(x, yp), 32, w), x_rs.at[k, 1])
-        p, q = rows(b, a_off(x, ym), 16, w), rows(b, a_off(x, yp) + 16, 16, w)
+        got(rows(b, a_off(x, ym), 32, wa), x_rs.at[k, 0])
+        got(rows(b, a_off(x, yp), 32, wa), x_rs.at[k, 1])
+        p, q = rows(b, a_off(x, ym), 16, wa), rows(b, a_off(x, yp) + 16, 16, wa)
         send(p, p, x_ss.at[k, 2], x_rs.at[k, 2], {"y": yp})
         send(q, q, x_ss.at[k, 3], x_rs.at[k, 3], {"y": ym})
-        got(rows(b, b_off(xm, y), 32, w), x_rs.at[k, 8])
-        got(rows(b, b_off(xp, y), 32, w), x_rs.at[k, 9])
-        p, q = rows(b, b_off(xm, y), 16, w), rows(b, b_off(xp, y) + 16, 16, w)
+        got(rows(b, b_off(xm, y), 32, wb), x_rs.at[k, 8])
+        got(rows(b, b_off(xp, y), 32, wb), x_rs.at[k, 9])
+        p, q = rows(b, b_off(xm, y), 16, wb), rows(b, b_off(xp, y) + 16, 16, wb)
         send(p, p, x_ss.at[k, 10], x_rs.at[k, 10], {"x": xp})
         send(q, q, x_ss.at[k, 11], x_rs.at[k, 11], {"x": xm})
 
-    def s3(k, w=384):
+    def s3(k, wa, wb):
         b = zblk(k)
         y2, x2 = (y + 2) % 4, (x + 2) % 4
-        got(rows(b, a_off(x, y2), 16, w), x_rs.at[k, 2])
-        got(rows(b, a_off(x, y2) + 16, 16, w), x_rs.at[k, 3])
-        p = rows(b, a_off(x, 0), 128, w)
+        got(rows(b, a_off(x, y2), 16, wa), x_rs.at[k, 2])
+        got(rows(b, a_off(x, y2) + 16, 16, wa), x_rs.at[k, 3])
+        p = rows(b, a_off(x, 0), 128, wa)
         send(p, p, x_ss.at[k, 4], x_rs.at[k, 4], {"x": xp})
         send(p, p, x_ss.at[k, 5], x_rs.at[k, 5], {"x": xm})
-        got(rows(b, b_off(x2, y), 16, w), x_rs.at[k, 10])
-        got(rows(b, b_off(x2, y) + 16, 16, w), x_rs.at[k, 11])
-        p = rows(b, b_off(0, y), 128, w)
+        got(rows(b, b_off(x2, y), 16, wb), x_rs.at[k, 10])
+        got(rows(b, b_off(x2, y) + 16, 16, wb), x_rs.at[k, 11])
+        p = rows(b, b_off(0, y), 128, wb)
         send(p, p, x_ss.at[k, 12], x_rs.at[k, 12], {"y": yp})
         send(p, p, x_ss.at[k, 13], x_rs.at[k, 13], {"y": ym})
 
-    def s4(k, w=384):
+    def s4(k, wa, wb):
         b = zblk(k)
-        got(rows(b, a_off(xm, 0), 128, w), x_rs.at[k, 4])
-        got(rows(b, a_off(xp, 0), 128, w), x_rs.at[k, 5])
-        p, q = rows(b, a_off(xm, 0), 64, w), rows(b, a_off(xp, 2), 64, w)
+        got(rows(b, a_off(xm, 0), 128, wa), x_rs.at[k, 4])
+        got(rows(b, a_off(xp, 0), 128, wa), x_rs.at[k, 5])
+        p, q = rows(b, a_off(xm, 0), 64, wa), rows(b, a_off(xp, 2), 64, wa)
         send(p, p, x_ss.at[k, 6], x_rs.at[k, 6], {"x": xp})
         send(q, q, x_ss.at[k, 7], x_rs.at[k, 7], {"x": xm})
-        got(rows(b, b_off(0, ym), 128, w), x_rs.at[k, 12])
-        got(rows(b, b_off(0, yp), 128, w), x_rs.at[k, 13])
-        p, q = rows(b, b_off(0, ym), 64, w), rows(b, b_off(2, yp), 64, w)
+        got(rows(b, b_off(0, ym), 128, wb), x_rs.at[k, 12])
+        got(rows(b, b_off(0, yp), 128, wb), x_rs.at[k, 13])
+        p, q = rows(b, b_off(0, ym), 64, wb), rows(b, b_off(2, yp), 64, wb)
         send(p, p, x_ss.at[k, 14], x_rs.at[k, 14], {"y": yp})
         send(q, q, x_ss.at[k, 15], x_rs.at[k, 15], {"y": ym})
 
-    def s5(k, w=384):
+    def s5(k, wa, wb):
         b = zblk(k)
         y2, x2 = (y + 2) % 4, (x + 2) % 4
-        got(rows(b, a_off(x2, 0), 64, w), x_rs.at[k, 6])
-        got(rows(b, a_off(x2, 2), 64, w), x_rs.at[k, 7])
-        got(rows(b, b_off(0, y2), 64, w), x_rs.at[k, 14])
-        got(rows(b, b_off(2, y2), 64, w), x_rs.at[k, 15])
+        got(rows(b, a_off(x2, 0), 64, wa), x_rs.at[k, 6])
+        got(rows(b, a_off(x2, 2), 64, wa), x_rs.at[k, 7])
+        got(rows(b, b_off(0, y2), 64, wb), x_rs.at[k, 14])
+        got(rows(b, b_off(2, y2), 64, wb), x_rs.at[k, 15])
 
     def send_kernel():
         kc = y % 2
@@ -374,39 +396,65 @@
         else:
             push_t(7, lo)
 
+    def pumped(t):
+        return jnp.clip(2 * (t - 4), 0, 16)
+
+    def pair(f, n):
+        @pl.when(n < 4)
+        def _():
+            f(2 * n - 1, 512, 384)
+            f(2 * n, 384, 512)
+
+        @pl.when(n == 4)
+        def _():
+            f(7, 512, 512)
+
+    def single(f, k):
+        @pl.when((k % 2 == 1) & (k < 7))
+        def _():
+            f(k, 512, 384)
+
+        @pl.when(k % 2 == 0)
+        def _():
+            f(k, 384, 512)
+
+        @pl.when(k == 7)
+        def _():
+            f(k, 512, 512)
+
     def tick(t, _):
         for s in range(1, 5):
             on(t == s, "forward", forward, s)
-        on(t == 4, "s5", s5, 0, 512)
-        on(t > 4, "s5", s5, t - 4)
+        on(t == 4, "s5", s5, 0, 512, 512)
+        on(t >= 7, "s5", single, s5, t - 6)
         for s in range(5):
             on(t == s, "c_step", c_step, s)
-        on(t == 3, "s4", s4, 0, 512)
-        on((t > 3) & (t < 11), "s4", s4, t - 3)
-        on(t == 2, "s3", s3, 0, 512)
-        on((t > 2) & (t < 10), "s3", s3, t - 2)
-        on(t == 1, "s2", s2, 0, 512)
-        on((t > 1) & (t < 9), "s2", s2, t - 1)
-        on(t == 0, "s1", s1, 0, 512)
-        on((t > 0) & (t < 8), "s1", s1, t)
+        on(t == 3, "s4", s4, 0, 512, 512)
+        on((t >= 5) & (t < 12), "s4", single, s4, t - 4)
+        on(t == 2, "s3", s3, 0, 512, 512)
+        on((t >= 3) & (t < 10), "s3", single, s3, t - 2)
+        on(t == 0, "s1", s1, 0, 512, 512)
+        on((t >= 1) & (t < 5), "s1", pair, s1, t)
         on(t == 0, "send_kernel", send_kernel)
         for s in range(1, 5):
             on(t == s, "forward_t", forward_t, s)
+        on(t == 3, "quarter", quarter_send, 0, 0, (z, z))
+        on(t == 4, "quarter", quarter_send, 0, 1, (z, z))
+        on(t == 4, "quarter", quarter_send, 0, 3, (z, z))
+        on(t == 4, "quarter", quarter_send, 0, 2, (z, z))
         on(t == 4, "make_half", make_half)
-        for s in range(5, 8):
-            on(t == 2 * s - 4, "c_step", c_step, s)
+        on(t == 1, "s2", s2, 0, 512, 512)
+        on((t >= 2) & (t < 4), "s2", pair, s2, t - 1)
+        on(t == 5, "s2", pair, s2, t - 2)
+        on(t == 5, "s2", pair, s2, t - 1)
+        with jax.named_scope("pump"):
+            lax.fori_loop(pumped(t - 1), pumped(t), pump, 0)
         on(t == READY, "take_half", take_half)
         with jax.named_scope("compute"):
-            lo = jnp.maximum(t - READY, 0)
-            hi = jnp.maximum(t - READY + 1, 0) + (t >= 11).astype(jnp.int32)
-            lax.fori_loop(lo, hi, compute, 0)
+            lax.fori_loop(jnp.maximum(t - READY, 0), jnp.maximum(t - READY + 1, 0), compute, 0)
         return 0
 
     lax.fori_loop(0, TICKS, tick, 0)
-    with jax.named_scope('c_step'):
-        c_step(8)
-    with jax.named_scope('compute'):
-        compute(7, 0)
 
     mine = pl.ds(pl.multiple_of(256 * c, 256), 256)
     give = acc.at[pl.ds(pl.multiple_of(256 * (1 - c), 256), 256)]
@@ -597,13 +645,13 @@
         for d in range(2):
             i = 2 * s + d
             if s < 3:
-                left(rows(0, 0, 32, 384), r_ss.at[i])
-                left(rows(0, 0, 32, 384), r_ss.at[8 + i])
+                left(rows(0, 0, 32, 512 if d else 384), r_ss.at[i])
+                left(rows(0, 0, 32, 384 if d else 512), r_ss.at[8 + i])
                 left(tt.at[0], t_ss.at[i])
                 for ch in range(2):
                     left(la_part(0, 0, ch), g_ss.at[i, ch])
             else:
-                left(rows(0, 0, 32, 384), r_ss.at[i])
+                left(rows(0, 0, 32), r_ss.at[i])
                 left(tt.at[0, pl.ds(0, 48 - 16 * d)], t_ss.at[i])
                 left(la_part(0, 0, d), g_ss.at[i, d])
     for n in range(8):
@@ -617,18 +665,23 @@
         left(rows(0, 0, 64), c_ss.at[4 + n])
         left(rows(0, 0, 32), c_ss.at[6 + n])
         for g in range(4):
-            for p, i in c_ring(g, n, 0):
-                left(p, c_ss.at[i])
-
-    def drain(k, w):
-        for o in (0, 8):
+            for q in range(4):
+                left(rows(0, 0, 96 if g < 3 else 32), e_ss.at[g, q, n])
+
+    def drain(k, wa, wb):
+        for o, w in ((0, wa), (8, wb)):
             for n, cnt in ((0, 32), (2, 16), (4, 128), (6, 64)):
                 left(rows(0, 0, cnt, w), x_ss.at[k, o + n])
                 left(rows(0, 0, cnt, w), x_ss.at[k, o + n + 1])
-        return w
-
-    drain(0, 512)
-    lax.fori_loop(1, 8, lambda k, _: drain(k, 384) * 0, 0)
+
+    def drain_two(n, _):
+        drain(2 * n + 1, 512, 384)
+        drain(2 * n + 2, 384, 512)
+        return 0
+
+    drain(0, 512, 512)
+    lax.fori_loop(0, 3, drain_two, 0)
+    drain(7, 512, 512)
 
     @pl.when(c == y % 2)
     def _():
@@ -693,7 +746,8 @@
             V((16, 8, 128), F32),
             V((8, 8, 128), F32),
             dma((8, 16)), dma((8, 16)),
-            dma((24,)), dma((24,)),
+            dma((4, 4, 2)), dma((4, 4, 2)),
+            dma((8,)), dma((8,)),
             dma((16,)), dma((16,)),
             dma((8,)), dma((8,)),
             dma((8,)), dma((8,)),

time: 149 us -> 135 us (0.906)
  Pallas kernels: 142 us -> 128 us
    pallas_call x1, Pallas kernels: 142 us -> 128 us  [shards(): pl.pallas_call(ladder_kernel, out_shape=(jax.ShapeDtypeStruct((600, 1200)...]
where the time goes in v4:
time: 135 us
  Pallas kernels  128 us (95%)
  local copies, waits for them, and re-layouts  5 us (4%)
  between operations  2.44 us (2%)
    pallas_call x1, Pallas kernels, shards(): pl.pallas_call(ladder_kernel, out_shape=(jax.ShapeDtypeStruct((600, 1200)...  128 us
    unnamed x1, local copies, waits for them, and re-layouts  3.71 us

profile of v4, /device:TPU:1, one launch (start us, length us, event | category | flops | bytes accessed | tf_op | source)
XLA Modules:
  0.0 135.1 jit_solution(350439607460981923)
XLA Ops:
  0.6 1.3 broadcast_in_dim.3.e_ref
  1.9 127.7 %ladder.1 = (f32[600,1200]{1,0:T(8,128)}, f32[1,1]{1,0:T(1,128)}) custom-call(bf16[75,512]{1,0:T(8,128)(2,1)} %f_ref.1, bf16[600,75]{1,0:T(8,128)(2,1)} %bitcast.12, bf16[512,512]{1,0:T(8,128)(2,1)} %k_ref.1, f32[600,1200]{1,0:T(8,128)} %bitcast.10, f32[1,1200]{1,0:T(1,128)} %broadcast_in_dim.3.e_ref, f32[8]{0:T(128)} %ep_ref.1), custom_call_target="tpu_custom_call" | custom-call | tf_op jit(solution)/shard_map/ladder/pallas_call | solution.py:713
  129.6 3.7 %copy.10 = f32[8,75,1200]{2,0,1:T(8,128)} copy(f32[8,75,1200]{2,0,1:T(8,128)} %bitcast.11) | data formatting | bytes 5760000

commit v5 on v4

--- a/solution.py
+++ b/solution.py
@@ -16,6 +16,8 @@
 TN = (((0,), (0,)), ((), ()))
 TICKS = 14
 READY = 6
+REGION = (pl.ds(1024, 256), pl.ds(0, 512), pl.ds(512, 512))
+PIECES = ((64, 16), (0, 32), (32, 32))
 FAR = sorted(((i, j) for i in range(4) for j in range(4) if i or j), key=lambda p: -min(p[0], 4 - p[0]) - min(p[1], 4 - p[1]))
 
 
@@ -25,10 +27,11 @@
 
 
 def ladder_kernel(
-    f_ref, t_ref, k_ref, other_hbm, e_ref, ep_ref, out_ref, rms_ref,
-    stage, res, zt_ref, er,
+    f_hbm, t_hbm, k_hbm, other_hbm, e_hbm, ep_hbm, out_ref, rms_ref,
+    f_ref, t_ref, k_ref, e_ref, ep_ref,
+    stage, res, packed, zt_ref, er,
     xb, tt, ttp, half, hs, hb, ht, zb_ref, wt, acc, rb, bs, br, ls, lb, lt, ltr, lc, la, sc, sp, sz,
-    x_ss, x_rs, e_ss, e_rs, c_ss, c_rs, r_ss, r_rs, t_ss, t_rs, u_ss, u_rs, g_ss, g_rs, m_ss, m_rs, p_ss, p_rs, q_ss, q_rs, loc,
+    x_ss, x_rs, e_ss, e_rs, c_ss, c_rs, r_ss, r_rs, t_ss, t_rs, u_ss, u_rs, g_ss, g_rs, h_ss, h_rs, m_ss, m_rs, d_ss, d_rs, p_ss, p_rs, q_ss, q_rs, loc,
 ):
     x, y, z, c = (lax.axis_index(n) for n in ("x", "y", "z", "core"))
     v = 4 * x + y
@@ -64,15 +67,14 @@
     def c_off(i, j):
         return 1024 + i * 64 + j * 16
 
-    own = [
-        pltpu.make_async_copy(f_ref.at[pl.ds(0, 32)], rows(z, a_off(x, y), 32), loc.at[0]),
-        pltpu.make_async_copy(f_ref.at[pl.ds(32, 32)], rows(z, b_off(x, y), 32), loc.at[1]),
+    loads = [
+        pltpu.make_async_copy(a, b, loc.at[n])
+        for n, (a, b) in enumerate(
+            ((f_hbm, f_ref), (t_hbm, t_ref), (k_hbm, k_ref), (e_hbm, e_ref), (ep_hbm, ep_ref), (other_hbm, stage))
+        )
     ]
-    for o in own:
+    for o in loads:
         o.start()
-
-    others = pltpu.make_async_copy(other_hbm, stage, loc.at[2])
-    others.start()
 
     bar = pltpu.get_barrier_semaphore()
 
@@ -94,8 +96,12 @@
 
     lax.fori_loop(1, 8, greet_z, 0)
     with jax.named_scope("local"):
+        loads[0].wait()
+        xb[z, pl.ds(pl.multiple_of(a_off(x, y), 16), 32), :] = f_ref[pl.ds(0, 32), :]
+        xb[z, pl.ds(pl.multiple_of(b_off(x, y), 16), 32), :] = f_ref[pl.ds(32, 32), :]
         last = jnp.concatenate([f_ref[pl.ds(64, 11), :].astype(F32), jnp.zeros((5, 512), F32)], 0)
         xb[z, pl.ds(pl.multiple_of(c_off(x, y), 16), 16), :] = last.astype(BF)
+        loads[1].wait()
         for n in range(5):
             cnt = 128 if n < 4 else 88
             m = t_ref[pl.ds(128 * n, cnt), :].astype(F32)
@@ -103,16 +109,16 @@
                 m = jnp.concatenate([m, jnp.zeros((128 - cnt, 75), F32)], 0)
             m = jnp.concatenate([m.T, jnp.zeros((5, 128), F32)], 0)
             tt[2 * z + c, :, pl.ds(128 * n, 128)] = m.astype(BF)
+        loads[2].wait()
         for n in range(4):
             zt_ref[:, pl.ds(128 * n, 128)] = k_ref[pl.ds(128 * n, 128), :].astype(F32).T.astype(BF)
-        er[:, pl.ds(0, 1200)] = jnp.broadcast_to(e_ref[...], (8, 1200))
+        for o in loads[3:]:
+            o.wait()
+        er[:, pl.ds(0, 1200)] = jnp.broadcast_to(e_ref[...].reshape(1, 1200), (8, 1200))
         er[:, pl.ds(1200, 80)] = jnp.zeros((8, 80), F32)
-        others.wait()
         for n in range(10):
             w = 128 if n < 9 else 48
             res[n, :, pl.ds(0, w)] = stage[:, pl.ds(128 * n, w)]
-    for o in own:
-        o.wait()
     with jax.named_scope('barrier'):
         pl.semaphore_wait(bar, 38)
 
@@ -330,15 +336,17 @@
                         for k in range(1, 4):
                             m = jnp.where(lanes == k, roll(part[k], (k - s) * 32), m)
                         hs[8 * a + 4 * h + s, :, pl.ds(128 * g, 128)] = m.astype(BF)
+            for s in range(8):
+                w = 8 * a + s
+
+                @pl.when(w != v)
+                def _(w=w):
+                    dev = {"x": w // 4, "y": w % 4}
+                    send(hs.at[w], hb.at[c, v], m_ss.at[1], m_rs.at[1], dev)
+
             return 0
 
         lax.fori_loop(0, 2, chunk, 0)
-
-        def one(j, _):
-            send(hs.at[(v + j) % 16], hb.at[c, v], m_ss.at[1], m_rs.at[1], plane_dev(j, c))
-            return 0
-
-        lax.fori_loop(1, 16, one, 0)
         pltpu.make_async_copy(hs.at[v], hb.at[c, v], m_rs.at[1]).start()
 
     def take_half():
@@ -361,7 +369,10 @@
         with jax.named_scope('w_zb'):
             got(zb_ref, m_rs.at[0])
 
-    def compute(k, _):
+    mine = pl.ds(pl.multiple_of(256 * c, 256), 256)
+    yours = pl.ds(pl.multiple_of(256 * (1 - c), 256), 256)
+
+    def compute(k, last):
         b = zblk(k)
         for q in range(2):
             q = pl.ds(256 * q, 256)
@@ -371,9 +382,12 @@
                 for i in range(8):
                     o = 256 * s + 32 * i
                     wt[pl.ds(o, 32), q] = (cp[o : o + 32] * zz[s]).astype(BF)
-        for a in range(5):
-            a = pl.ds(256 * a, 256)
+        for n in (4, 0, 1, 2, 3):
+            a = pl.ds(256 * n, 256)
             acc[:, a] += lax.dot_general(wt[...], xb[b, a, :], NT, preferred_element_type=F32)
+            if last is True and (n % 2 or n == 4):
+                h = (n // 2 + 1) % 3
+                send(acc.at[yours, REGION[h]], rb.at[:, REGION[h]], d_ss.at[h], d_rs.at[h], sib)
         return 0
 
     def on(cond, name, f, *args):
@@ -429,10 +443,11 @@
         on(t >= 7, "s5", single, s5, t - 6)
         for s in range(5):
             on(t == s, "c_step", c_step, s)
+        on(t == READY, "take_half", take_half)
         on(t == 3, "s4", s4, 0, 512, 512)
         on((t >= 5) & (t < 12), "s4", single, s4, t - 4)
         on(t == 2, "s3", s3, 0, 512, 512)
-        on((t >= 3) & (t < 10), "s3", single, s3, t - 2)
+        on((t >= 3) & (t < 10) & (t != 4), "s3", single, s3, t - 2)
         on(t == 0, "s1", s1, 0, 512, 512)
         on((t >= 1) & (t < 5), "s1", pair, s1, t)
         on(t == 0, "send_kernel", send_kernel)
@@ -443,47 +458,37 @@
         on(t == 4, "quarter", quarter_send, 0, 3, (z, z))
         on(t == 4, "quarter", quarter_send, 0, 2, (z, z))
         on(t == 4, "make_half", make_half)
+        on(t == 4, "s3", s3, 2, 384, 512)
         on(t == 1, "s2", s2, 0, 512, 512)
         on((t >= 2) & (t < 4), "s2", pair, s2, t - 1)
         on(t == 5, "s2", pair, s2, t - 2)
-        on(t == 5, "s2", pair, s2, t - 1)
+        on(t == 7, "s2", s2, 7, 512, 512)
         with jax.named_scope("pump"):
             lax.fori_loop(pumped(t - 1), pumped(t), pump, 0)
-        on(t == READY, "take_half", take_half)
         with jax.named_scope("compute"):
-            lax.fori_loop(jnp.maximum(t - READY, 0), jnp.maximum(t - READY + 1, 0), compute, 0)
+            lax.fori_loop(jnp.maximum(t - READY, 0), jnp.where(t < TICKS - 1, jnp.maximum(t - READY + 1, 0), 7), compute, 0)
         return 0
 
     lax.fori_loop(0, TICKS, tick, 0)
-
-    mine = pl.ds(pl.multiple_of(256 * c, 256), 256)
-    give = acc.at[pl.ds(pl.multiple_of(256 * (1 - c), 256), 256)]
-    send(give, rb, m_ss.at[3], m_rs.at[3], sib)
-    with jax.named_scope('w_rb'):
-        got(rb, m_rs.at[3])
-    for n in range(10):
-        a = pl.ds(128 * n, 128)
-        m = (acc[mine, a] + rb[:, a]).T.astype(BF)
-        if n < 4:
-            for j in range(4):
-                bs[4 * n + j, pl.ds(0, 32), :] = m[32 * j : 32 * j + 32]
-        elif n < 8:
-            for j in range(4):
-                bs[4 * j + n - 4, pl.ds(32, 32), :] = m[32 * j : 32 * j + 32]
-        else:
-            for j in range(8):
-                bs[8 * (n - 8) + j, pl.ds(64, 16), :] = m[16 * j : 16 * j + 16]
-
-    pieces = ((0, 32), (32, 48))
-    for h, (lo, n) in enumerate(pieces):
-
+    with jax.named_scope('compute'):
+        compute(7, True)
+
+    for h, (lo, cnt) in enumerate(PIECES):
+        with jax.named_scope("w_rb"):
+            got(rb.at[:, REGION[h]], d_rs.at[h])
+        for n in (range(8, 10), range(4), range(4, 8))[h]:
+            a = pl.ds(128 * n, 128)
+            m = (acc[mine, a] + rb[:, a]).T.astype(BF)
+            for j in range(128 // cnt):
+                w = (8 * (n - 8) + j, 4 * n + j, 4 * j + n - 4)[h]
+                bs[w, pl.ds(lo, cnt), :] = m[cnt * j : cnt * j + cnt]
         for i, j in FAR:
             i, j = (x + i) % 4, (y + j) % 4
             w = 4 * i + j
-            send(bs.at[w, pl.ds(lo, n)], br.at[v, pl.ds(lo, n)], p_ss.at[h], p_rs.at[h], {"x": i, "y": j})
-        pltpu.make_async_copy(bs.at[v, pl.ds(lo, n)], br.at[v, pl.ds(lo, n)], p_rs.at[h]).start()
-
-    for h, (lo, n) in enumerate(pieces):
+            send(bs.at[w, pl.ds(lo, cnt)], br.at[v, pl.ds(lo, cnt)], p_ss.at[h], p_rs.at[h], {"x": i, "y": j})
+        pltpu.make_async_copy(bs.at[v, pl.ds(lo, cnt)], br.at[v, pl.ds(lo, cnt)], p_rs.at[h]).start()
+
+    for h, (lo, n) in enumerate(PIECES):
         with jax.named_scope("w_br"):
             got(br.at[:, pl.ds(lo, n)], p_rs.at[h])
         with jax.named_scope("unpack"):
@@ -496,7 +501,7 @@
                         for s in range(1, 4):
                             m = jnp.where(lanes == s, roll(part[s], (s - k) * 32), m)
                         ls[4 * g + k, pl.ds(lo, n), pl.ds(128 * a, 128)] = m.astype(BF)
-        for d in (4, 3, 5, 2, 6, 1, 7):
+        for d in (7, 1, 6, 2, 5, 3, 4):
             w = (z + d) % 8
             send(ls.at[w, pl.ds(lo, n)], lb.at[z, pl.ds(lo, n)], q_ss.at[h, d], q_rs.at[h, d], {"z": w})
         if h == 0:
@@ -510,10 +515,10 @@
     lad(z, ls)
 
     def lad_step(j, _):
-        d = 4 + ((j + 1) // 2) * (1 - 2 * (j % 2))
+        d = 4 + ((7 - j) // 2) * (1 - 2 * (j % 2))
         b = (z + 8 - d) % 8
         with jax.named_scope("w_lb"):
-            for h, (lo, n) in enumerate(pieces):
+            for h, (lo, n) in enumerate(PIECES):
                 got(lb.at[b, pl.ds(lo, n)], q_rs.at[h, d])
         with jax.named_scope("w_lad"):
             lad(b, lb)
@@ -534,21 +539,22 @@
         b = pl.ds(128 * n, 128)
         la[z, :, b] = lc[b, :].T[:80].astype(BF)
 
-    chunks = ((0, 48), (48, 32))
-
-    def la_part(i, h, ch):
-        lo, n = chunks[ch]
+
+    def la_part(i, h, lo, n=16):
         return la.at[i, pl.ds(lo, n), pl.ds(pl.multiple_of(640 * h, 128), 640)]
 
     def la_send(s, blk, d, ch):
-        p = la_part(blk, c, ch)
-        send(p, p, g_ss.at[2 * s + d, ch], g_rs.at[2 * s + d, ch], {"z": (zp, zm)[d]})
-
-    def la_push(n, blk, ch):
-        p = la_part(blk, c, ch)
-        send(p, p, g_ss.at[8 + n, ch], g_rs.at[8 + n, ch], sib)
-
-    for ch in range(2):
+        p = la_part(blk, c, 16 * ch)
+        dev = {"z": ((zp, zm)[d] if s < 3 else (z + (2, 6)[d]) % 8)}
+        send(p, p, g_ss.at[2 * s + d, ch], g_rs.at[2 * s + d, ch], dev)
+
+    HALF = ((0, 48), (48, 32))
+
+    def la_push(n, blk, h):
+        p = la_part(blk, c, *HALF[h])
+        send(p, p, h_ss.at[n, h], h_rs.at[n, h], sib)
+
+    for ch in range(5):
         for d in range(2):
             la_send(0, z, d, ch)
 
@@ -576,28 +582,32 @@
         o = pl.ds(i, 75, stride=8)
         for n in range(10):
             b = pl.ds(128 * n, 128)
-            res[n, o, :] = res[n, o, :] + la[i, :, b].astype(F32)[:75]
+            res[n, o, :] = la[i, :, b].astype(F32)[:75]
 
     for s in range(4):
         lo, hi = (z + 7 - s) % 8, (z + 1 + s) % 8
         with jax.named_scope(f"w_la{s}"):
-            if s < 3:
-                for ch in range(2):
-                    got(la_part(lo, c, ch), g_rs.at[2 * s, ch])
-                    if s < 2 or ch == 0:
+            for ch in range(5):
+                if s < 3:
+                    got(la_part(lo, c, 16 * ch), g_rs.at[2 * s, ch])
+                    if s < 2:
                         la_send(s + 1, lo, 0, ch)
-                    la_push(2 * s + 1, lo, ch)
-                    got(la_part(hi, c, ch), g_rs.at[2 * s + 1, ch])
-                    if s < 2 or ch == 1:
+                    if s == 1 and ch < 3:
+                        la_send(3, lo, 0, ch)
+                    got(la_part(hi, c, 16 * ch), g_rs.at[2 * s + 1, ch])
+                    if s < 2:
                         la_send(s + 1, hi, 1, ch)
-                    la_push(2 * s, hi, ch)
-            else:
-                for ch in range(2):
-                    got(la_part(lo, c, ch), g_rs.at[6 + ch, ch])
-                    la_push(6, lo, ch)
+                    if s == 1 and ch >= 3:
+                        la_send(3, hi, 1, ch)
+                else:
+                    got(la_part(lo, c, 16 * ch), g_rs.at[6 + (ch >= 3), ch])
+                if ch in (2, 4):
+                    h = ch // 2 - 1
+                    la_push(2 * s + (s < 3), lo, h)
+                    if s < 3:
+                        la_push(2 * s, hi, h)
         if s == 0:
             finish(z)
-        if s == 1:
             with jax.named_scope("w_sp"):
                 got(sp, m_rs.at[7])
             s_all = sp[0]
@@ -614,21 +624,21 @@
             for n in (2 * s - 2, 2 * s - 1):
                 with jax.named_scope("w_las"):
                     for ch in range(2):
-                        got(la_part(zblk(n + 1), 1 - c, ch), g_rs.at[8 + n, ch])
+                        got(la_part(zblk(n + 1), 1 - c, *HALF[ch]), h_rs.at[n, ch])
                 with jax.named_scope("finish"):
                     finish(zblk(n + 1))
     with jax.named_scope("w_las"):
         for ch in range(2):
-            got(la_part(zblk(7), 1 - c, ch), g_rs.at[14, ch])
+            got(la_part(zblk(7), 1 - c, *HALF[ch]), h_rs.at[6, ch])
     with jax.named_scope("finish"):
         finish(zblk(7))
     outs = []
-    for lo in range(0, 600, 200):
+    for h, (lo, cnt) in enumerate(((0, 208), (208, 208), (416, 184))):
+        p = pl.ds(lo, cnt)
         for n in range(10):
             w = 128 if n < 9 else 48
-            stage[pl.ds(lo, 200), pl.ds(128 * n, w)] = res[n, pl.ds(lo, 200), pl.ds(0, w)]
-        p = pl.ds(lo, 200)
-        outs.append(pltpu.make_async_copy(stage.at[p], out_ref.at[p], loc.at[3 + lo // 200]))
+            packed[p, pl.ds(128 * n, w)] = res[n, p, pl.ds(0, w)].astype(BF)
+        outs.append(pltpu.make_async_copy(packed.at[p], out_ref.at[p], loc.at[3 + h]))
         outs[-1].start()
     with jax.named_scope("w_sz"):
         got(sz.at[pl.ds(0, 7)], m_rs.at[8])
@@ -648,17 +658,18 @@
                 left(rows(0, 0, 32, 512 if d else 384), r_ss.at[i])
                 left(rows(0, 0, 32, 384 if d else 512), r_ss.at[8 + i])
                 left(tt.at[0], t_ss.at[i])
-                for ch in range(2):
-                    left(la_part(0, 0, ch), g_ss.at[i, ch])
+                for ch in range(5):
+                    left(la_part(0, 0, 0), g_ss.at[i, ch])
             else:
                 left(rows(0, 0, 32), r_ss.at[i])
                 left(tt.at[0, pl.ds(0, 48 - 16 * d)], t_ss.at[i])
-                left(la_part(0, 0, d), g_ss.at[i, d])
+                for ch in ((0, 1, 2), (3, 4))[d]:
+                    left(la_part(0, 0, 0), g_ss.at[i, ch])
     for n in range(8):
         left(tt.at[0], u_ss.at[n])
     for n in range(7):
         for ch in range(2):
-            left(la_part(0, 0, ch), g_ss.at[8 + n, ch])
+            left(la_part(0, 0, *HALF[ch]), h_ss.at[n, ch])
     for n in (0, 1):
         left(rows(0, 0, 16), c_ss.at[n])
         left(xb.at[0, pl.ds(0, 16), pl.ds(0, 256)], c_ss.at[2 + n])
@@ -693,8 +704,9 @@
 
     left(hs.at[pl.ds(0, 15)], m_ss.at[1])
     left(hb.at[0], m_ss.at[2])
-    left(rb, m_ss.at[3])
-    for h, (lo, n) in enumerate(pieces):
+    for h in range(3):
+        left(rb.at[:, REGION[h]], d_ss.at[h])
+    for h, (lo, n) in enumerate(PIECES):
         left(bs.at[pl.ds(0, 15), pl.ds(lo, n)], p_ss.at[h])
         for d in range(1, 8):
             left(ls.at[0, pl.ds(lo, n)], q_ss.at[h, d])
@@ -706,21 +718,26 @@
 def shards(amplitudes, factors, kernel, other_terms, virt_energy, pair_energy):
     t = jnp.transpose(amplitudes, (1, 0, 2)).reshape(600, 75)
     other = jnp.transpose(other_terms, (1, 0, 2)).reshape(600, 1200)
-    vm = pl.BlockSpec(memory_space=pltpu.VMEM)
     sm = pl.BlockSpec(memory_space=pltpu.SMEM)
     V = pltpu.VMEM
     dma = pltpu.SemaphoreType.DMA
     out, rms = pl.pallas_call(
         ladder_kernel,
         out_shape=(
-            jax.ShapeDtypeStruct((600, 1200), F32),
+            jax.ShapeDtypeStruct((600, 1200), BF),
             jax.ShapeDtypeStruct((1, 1), F32),
         ),
-        in_specs=[vm, vm, vm, pl.BlockSpec(memory_space=pl.ANY), vm, sm],
+        in_specs=[pl.BlockSpec(memory_space=pltpu.HBM)] * 6,
         out_specs=(pl.BlockSpec(memory_space=pl.ANY), sm),
         scratch_shapes=[
+            V((75, 512), BF),
+            V((600, 75), BF),
+            V((512, 512), BF),
+            V((1200,), F32),
+            pltpu.SMEM((8,), F32),
             V((600, 1200), F32),
             V((10, 600, 128), F32),
+            V((600, 1200), BF),
             V((512, 512), BF),
             V((8, 1280), F32),
             V((8, 1280, 512), BF),
@@ -751,18 +768,21 @@
             dma((16,)), dma((16,)),
             dma((8,)), dma((8,)),
             dma((8,)), dma((8,)),
-            dma((16, 2)), dma((16, 2)),
+            dma((8, 5)), dma((8, 5)),
+            dma((8, 2)), dma((8, 2)),
             dma((16,)), dma((16,)),
-            dma((2,)), dma((2,)),
-            dma((2, 8)), dma((2, 8)),
+            dma((3,)), dma((3,)),
+            dma((3,)), dma((3,)),
+            dma((3, 8)), dma((3, 8)),
             dma((12,)),
         ],
         compiler_params=pltpu.CompilerParams(
-            collective_id=0, has_side_effects=True, vmem_limit_bytes=60 * 1024 * 1024
+            collective_id=0, has_side_effects=True, vmem_limit_bytes=56 * 1024 * 1024
         ),
         name="ladder",
-    )(factors, t, kernel, other, virt_energy[None, :], pair_energy)
-    return jnp.transpose(out.reshape(75, 8, 1200), (1, 0, 2)), rms.reshape(())
+    )(factors, t, kernel, other, virt_energy, pair_energy)
+    residual = other + out.astype(F32)
+    return jnp.transpose(residual.reshape(75, 8, 1200), (1, 0, 2)), rms.reshape(())
 
 
 def solution(mesh):

time: 135 us -> 130 us (0.963)
  local copies, waits for them, and re-layouts: 5 us -> 0.01 us
  Pallas kernels: 128 us -> 124 us
  other arithmetic: 0 us -> 3.32 us
    unnamed x1 -> x2, local copies, waits for them, and re-layouts: 3.71 us -> 0.01 us
    pallas_call x1, Pallas kernels: 128 us -> 124 us  [shards(): pl.pallas_call(ladder_kernel, out_shape=(jax.ShapeDtypeStruct((600, 1200)...]
    transpose x0 -> x1, other arithmetic: none -> 3.32 us  [shards(): jnp.transpose(residual.reshape(75, 8, 1200), (1, 0, 2))]
where the time goes in v5:
time: 130 us
  Pallas kernels  124 us (95%)
  other arithmetic  3.32 us (3%)
  between operations  2.39 us (2%)
    pallas_call x1, Pallas kernels, shards(): pl.pallas_call(ladder_kernel, out_shape=(jax.ShapeDtypeStruct((600, 1200)...  124 us
    transpose x1, other arithmetic, shards(): jnp.transpose(residual.reshape(75, 8, 1200), (1, 0, 2))  3.32 us

profile of v5, /device:TPU:1, one launch (start us, length us, event | category | flops | bytes accessed | tf_op | source)
XLA Modules:
  0.0 129.8 jit_solution(6982392065982097124)
XLA Ops:
  0.6 0.0 copy-start
  0.6 124.1 %ladder.1 = (bf16[600,1200]{1,0:T(8,128)(2,1)}, f32[1,1]{1,0:T(1,128)}) custom-call(bf16[75,512]{1,0:T(8,128)(2,1)} %f_hbm.1, bf16[600,75]{1,0:T(8,128)(2,1)} %bitcast.13, bf16[512,512]{1,0:T(8,128)(2,1)} %k_hbm.1, f32[600,1200]{1,0:T(8,128)} %bitcast.12, f32[1200]{0:T(1024)} %e_hbm.1, f32[8]{0:T(128)} %ep_hbm.1), custom_call_target="tpu_custom_call" | custom-call | tf_op jit(solution)/shard_map/ladder/pallas_call | solution.py:724
  124.7 0.0 copy-done
  124.7 3.3 %add_bitcast_fusion = f32[8,75,1200]{2,0,1:T(8,128)} fusion(bf16[600,1200]{1,0:T(8,128)(2,1)} %get-tuple-element.4, f32[8,75,1200]{2,0,1:T(8,128)S(1)} %copy-done), kind=kLoop, calls=%fused_computation | loop fusion | flops 1440000 | bytes 7200000 | tf_op jit(solution)/shard_map/transpose | solution.py:785
Async XLA Ops:
  0.6 124.1 %copy-start = (f32[8,75,1200]{2,0,1:T(8,128)S(1)}, f32[8,75,1200]{2,0,1:T(8,128)}, u32[]{:S(2)}) copy-start(f32[8,75,1200]{2,0,1:T(8,128)} %param.9) | copy-start | bytes 8640004

commit v6 on v5

--- a/solution.py
+++ b/solution.py
@@ -31,7 +31,7 @@
     f_ref, t_ref, k_ref, e_ref, ep_ref,
     stage, res, packed, zt_ref, er,
     xb, tt, ttp, half, hs, hb, ht, zb_ref, wt, acc, rb, bs, br, ls, lb, lt, ltr, lc, la, sc, sp, sz,
-    x_ss, x_rs, e_ss, e_rs, c_ss, c_rs, r_ss, r_rs, t_ss, t_rs, u_ss, u_rs, g_ss, g_rs, h_ss, h_rs, m_ss, m_rs, d_ss, d_rs, p_ss, p_rs, q_ss, q_rs, loc,
+    x_ss, x_rs, fin, e_rs, c_rs, r_rs, t_rs, u_rs, g_rs, h_rs, m_rs, d_rs, p_rs, q_rs, loc,
 ):
     x, y, z, c = (lax.axis_index(n) for n in ("x", "y", "z", "core"))
     v = 4 * x + y
@@ -137,16 +137,16 @@
     def ring_step(s, zl, zr):
         for d, blk in enumerate((zl, zr)):
             for p, i in ring_pieces(s, d, blk):
-                send(p, p, r_ss.at[i], r_rs.at[i], {"z": (zp, zm)[d]})
+                send(p, p, fin.at[0], r_rs.at[i], {"z": (zp, zm)[d]})
 
     def t_step(s, zl, zr):
         for d, blk in enumerate((zl, zr)):
             p = t_piece(s, d, blk)
-            send(p, p, t_ss.at[2 * s + d], t_rs.at[2 * s + d], {"z": (zp, zm)[d]})
+            send(p, p, fin.at[1], t_rs.at[2 * s + d], {"z": (zp, zm)[d]})
 
     def push_t(n, blk):
         r = 2 * blk + c
-        send(tt.at[r], tt.at[r], u_ss.at[n], u_rs.at[n], sib)
+        send(tt.at[r], tt.at[r], fin.at[2], u_rs.at[n], sib)
 
     def ring_got(s):
         lo, hi = (z + 7 - s) % 8, (z + 1 + s) % 8
@@ -171,26 +171,26 @@
     def c_step(s):
         if s == 0:
             p = rows(z, c_off(x, y), 16)
-            send(p, p, c_ss.at[0], c_rs.at[0], {"y": yp})
-            send(p, p, c_ss.at[1], c_rs.at[1], {"y": ym})
+            send(p, p, fin.at[3], c_rs.at[0], {"y": yp})
+            send(p, p, fin.at[3], c_rs.at[1], {"y": ym})
         elif s == 1:
             got(rows(z, c_off(x, ym), 16), c_rs.at[0])
             got(rows(z, c_off(x, yp), 16), c_rs.at[1])
             p, q = c_piece(x, ym, 0), c_piece(x, yp, 1)
-            send(p, p, c_ss.at[2], c_rs.at[2], {"y": yp})
-            send(q, q, c_ss.at[3], c_rs.at[3], {"y": ym})
+            send(p, p, fin.at[3], c_rs.at[2], {"y": yp})
+            send(q, q, fin.at[3], c_rs.at[3], {"y": ym})
         elif s == 2:
             got(c_piece(x, (y + 2) % 4, 0), c_rs.at[2])
             got(c_piece(x, (y + 2) % 4, 1), c_rs.at[3])
             p = rows(z, c_off(x, 0), 64)
-            send(p, p, c_ss.at[4], c_rs.at[4], {"x": xp})
-            send(p, p, c_ss.at[5], c_rs.at[5], {"x": xm})
+            send(p, p, fin.at[3], c_rs.at[4], {"x": xp})
+            send(p, p, fin.at[3], c_rs.at[5], {"x": xm})
         elif s == 3:
             got(rows(z, c_off(xm, 0), 64), c_rs.at[4])
             got(rows(z, c_off(xp, 0), 64), c_rs.at[5])
             p, q = rows(z, c_off(xm, 0), 32), rows(z, c_off(xp, 2), 32)
-            send(p, p, c_ss.at[6], c_rs.at[6], {"x": xp})
-            send(q, q, c_ss.at[7], c_rs.at[7], {"x": xm})
+            send(p, p, fin.at[3], c_rs.at[6], {"x": xp})
+            send(q, q, fin.at[3], c_rs.at[7], {"x": xm})
         else:
             got(rows(z, c_off((x + 2) % 4, 0), 32), c_rs.at[6])
             got(rows(z, c_off((x + 2) % 4, 2), 32), c_rs.at[7])
@@ -205,7 +205,7 @@
     def quarter_send(g, q, blks, half_only=False):
         for d, blk in enumerate(blks):
             for p in quarter(blk, q, d, half_only):
-                send(p, p, e_ss.at[g, q, d], e_rs.at[g, q, d], {"z": (zp, zm)[d]})
+                send(p, p, fin.at[4], e_rs.at[g, q, d], {"z": (zp, zm)[d]})
 
     def pump(e, _):
         g, i = e // 4, e % 4
@@ -238,57 +238,49 @@
         b = zblk(k)
         p, q = rows(b, a_off(x, y), 32, wa), rows(b, b_off(x, y), 32, wb)
         send(p, p, x_ss.at[k, 0], x_rs.at[k, 0], {"y": yp})
-        send(p, p, x_ss.at[k, 1], x_rs.at[k, 1], {"y": ym})
-        send(q, q, x_ss.at[k, 8], x_rs.at[k, 8], {"x": xp})
-        send(q, q, x_ss.at[k, 9], x_rs.at[k, 9], {"x": xm})
+        send(p, p, x_ss.at[k, 0], x_rs.at[k, 0], {"y": ym})
+        send(q, q, x_ss.at[k, 1], x_rs.at[k, 4], {"x": xp})
+        send(q, q, x_ss.at[k, 1], x_rs.at[k, 4], {"x": xm})
 
     def s2(k, wa, wb):
         b = zblk(k)
-        got(rows(b, a_off(x, ym), 32, wa), x_rs.at[k, 0])
-        got(rows(b, a_off(x, yp), 32, wa), x_rs.at[k, 1])
+        got(rows(b, 0, 64, wa), x_rs.at[k, 0])
         p, q = rows(b, a_off(x, ym), 16, wa), rows(b, a_off(x, yp) + 16, 16, wa)
-        send(p, p, x_ss.at[k, 2], x_rs.at[k, 2], {"y": yp})
-        send(q, q, x_ss.at[k, 3], x_rs.at[k, 3], {"y": ym})
-        got(rows(b, b_off(xm, y), 32, wb), x_rs.at[k, 8])
-        got(rows(b, b_off(xp, y), 32, wb), x_rs.at[k, 9])
+        send(p, p, x_ss.at[k, 0], x_rs.at[k, 1], {"y": yp})
+        send(q, q, x_ss.at[k, 0], x_rs.at[k, 1], {"y": ym})
+        got(rows(b, 0, 64, wb), x_rs.at[k, 4])
         p, q = rows(b, b_off(xm, y), 16, wb), rows(b, b_off(xp, y) + 16, 16, wb)
-        send(p, p, x_ss.at[k, 10], x_rs.at[k, 10], {"x": xp})
-        send(q, q, x_ss.at[k, 11], x_rs.at[k, 11], {"x": xm})
+        send(p, p, x_ss.at[k, 1], x_rs.at[k, 5], {"x": xp})
+        send(q, q, x_ss.at[k, 1], x_rs.at[k, 5], {"x": xm})
 
     def s3(k, wa, wb):
         b = zblk(k)
         y2, x2 = (y + 2) % 4, (x + 2) % 4
-        got(rows(b, a_off(x, y2), 16, wa), x_rs.at[k, 2])
-        got(rows(b, a_off(x, y2) + 16, 16, wa), x_rs.at[k, 3])
+        got(rows(b, 0, 32, wa), x_rs.at[k, 1])
         p = rows(b, a_off(x, 0), 128, wa)
-        send(p, p, x_ss.at[k, 4], x_rs.at[k, 4], {"x": xp})
-        send(p, p, x_ss.at[k, 5], x_rs.at[k, 5], {"x": xm})
-        got(rows(b, b_off(x2, y), 16, wb), x_rs.at[k, 10])
-        got(rows(b, b_off(x2, y) + 16, 16, wb), x_rs.at[k, 11])
+        send(p, p, x_ss.at[k, 0], x_rs.at[k, 2], {"x": xp})
+        send(p, p, x_ss.at[k, 0], x_rs.at[k, 2], {"x": xm})
+        got(rows(b, 0, 32, wb), x_rs.at[k, 5])
         p = rows(b, b_off(0, y), 128, wb)
-        send(p, p, x_ss.at[k, 12], x_rs.at[k, 12], {"y": yp})
-        send(p, p, x_ss.at[k, 13], x_rs.at[k, 13], {"y": ym})
+        send(p, p, x_ss.at[k, 1], x_rs.at[k, 6], {"y": yp})
+        send(p, p, x_ss.at[k, 1], x_rs.at[k, 6], {"y": ym})
 
     def s4(k, wa, wb):
         b = zblk(k)
-        got(rows(b, a_off(xm, 0), 128, wa), x_rs.at[k, 4])
-        got(rows(b, a_off(xp, 0), 128, wa), x_rs.at[k, 5])
+        got(rows(b, 0, 256, wa), x_rs.at[k, 2])
         p, q = rows(b, a_off(xm, 0), 64, wa), rows(b, a_off(xp, 2), 64, wa)
-        send(p, p, x_ss.at[k, 6], x_rs.at[k, 6], {"x": xp})
-        send(q, q, x_ss.at[k, 7], x_rs.at[k, 7], {"x": xm})
-        got(rows(b, b_off(0, ym), 128, wb), x_rs.at[k, 12])
-        got(rows(b, b_off(0, yp), 128, wb), x_rs.at[k, 13])
+        send(p, p, x_ss.at[k, 0], x_rs.at[k, 3], {"x": xp})
+        send(q, q, x_ss.at[k, 0], x_rs.at[k, 3], {"x": xm})
+        got(rows(b, 0, 256, wb), x_rs.at[k, 6])
         p, q = rows(b, b_off(0, ym), 64, wb), rows(b, b_off(2, yp), 64, wb)
-        send(p, p, x_ss.at[k, 14], x_rs.at[k, 14], {"y": yp})
-        send(q, q, x_ss.at[k, 15], x_rs.at[k, 15], {"y": ym})
+        send(p, p, x_ss.at[k, 1], x_rs.at[k, 7], {"y": yp})
+        send(q, q, x_ss.at[k, 1], x_rs.at[k, 7], {"y": ym})
 
     def s5(k, wa, wb):
         b = zblk(k)
         y2, x2 = (y + 2) % 4, (x + 2) % 4
-        got(rows(b, a_off(x2, 0), 64, wa), x_rs.at[k, 6])
-        got(rows(b, a_off(x2, 2), 64, wa), x_rs.at[k, 7])
-        got(rows(b, b_off(0, y2), 64, wb), x_rs.at[k, 14])
-        got(rows(b, b_off(2, y2), 64, wb), x_rs.at[k, 15])
+        got(rows(b, 0, 128, wa), x_rs.at[k, 3])
+        got(rows(b, 0, 128, wb), x_rs.at[k, 7])
 
     def send_kernel():
         kc = y % 2
@@ -296,7 +288,7 @@
         def one(j, _):
             w = (v + j) % 16
             src = zt_ref.at[pl.ds(pl.multiple_of(32 * w, 32), 32)]
-            send(src, zb_ref.at[v // 2, c], m_ss.at[0], m_rs.at[0], plane_dev(j, kc))
+            send(src, zb_ref.at[v // 2, c], fin.at[15], m_rs.at[0], plane_dev(j, kc))
             return 0
 
         lax.fori_loop(1, 16, one, 0)
@@ -308,7 +300,7 @@
 
         @pl.when(c != kc)
         def _():
-            send(src, zb_ref.at[v // 2, c], m_ss.at[0], m_rs.at[0], sib)
+            send(src, zb_ref.at[v // 2, c], fin.at[15], m_rs.at[0], sib)
 
     def make_half():
         for n in range(1, 8):
@@ -342,7 +334,7 @@
                 @pl.when(w != v)
                 def _(w=w):
                     dev = {"x": w // 4, "y": w % 4}
-                    send(hs.at[w], hb.at[c, v], m_ss.at[1], m_rs.at[1], dev)
+                    send(hs.at[w], hb.at[c, v], fin.at[5], m_rs.at[1], dev)
 
             return 0
 
@@ -352,7 +344,7 @@
     def take_half():
         with jax.named_scope('w_hb'):
             got(hb.at[c], m_rs.at[1])
-        send(hb.at[c], hb.at[c], m_ss.at[2], m_rs.at[2], sib)
+        send(hb.at[c], hb.at[c], fin.at[6], m_rs.at[2], sib)
         acc[...] = jnp.zeros_like(acc)
         with jax.named_scope('w_hbs'):
             got(hb.at[1 - c], m_rs.at[2])
@@ -387,7 +379,7 @@
             acc[:, a] += lax.dot_general(wt[...], xb[b, a, :], NT, preferred_element_type=F32)
             if last is True and (n % 2 or n == 4):
                 h = (n // 2 + 1) % 3
-                send(acc.at[yours, REGION[h]], rb.at[:, REGION[h]], d_ss.at[h], d_rs.at[h], sib)
+                send(acc.at[yours, REGION[h]], rb.at[:, REGION[h]], fin.at[7], d_rs.at[h], sib)
         return 0
 
     def on(cond, name, f, *args):
@@ -485,8 +477,29 @@
         for i, j in FAR:
             i, j = (x + i) % 4, (y + j) % 4
             w = 4 * i + j
-            send(bs.at[w, pl.ds(lo, cnt)], br.at[v, pl.ds(lo, cnt)], p_ss.at[h], p_rs.at[h], {"x": i, "y": j})
+            send(bs.at[w, pl.ds(lo, cnt)], br.at[v, pl.ds(lo, cnt)], fin.at[8], p_rs.at[h], {"x": i, "y": j})
         pltpu.make_async_copy(bs.at[v, pl.ds(lo, cnt)], br.at[v, pl.ds(lo, cnt)], p_rs.at[h]).start()
+
+    for k in range(8):
+        wa, wb = (512, 512) if k in (0, 7) else (512, 384) if k % 2 else (384, 512)
+        left(rows(0, 0, 480, wa), x_ss.at[k, 0])
+        left(rows(0, 0, 480, wb), x_ss.at[k, 1])
+    left(rows(0, 0, 400), fin.at[0])
+    left(tt.at[pl.ds(0, 7)], fin.at[1])
+    left(tt.at[pl.ds(0, 8)], fin.at[2])
+    left(rows(0, 0, 240), fin.at[3])
+    left(xb.at[pl.ds(0, 2)], fin.at[4])
+    left(hs.at[pl.ds(0, 15)], fin.at[5])
+    left(hb.at[0], fin.at[6])
+    left(rb, fin.at[7])
+
+    @pl.when(c == y % 2)
+    def _():
+        left(zt_ref.at[pl.ds(0, 480)], fin.at[15])
+
+    @pl.when(c != y % 2)
+    def _():
+        left(zt_ref, fin.at[15])
 
     for h, (lo, n) in enumerate(PIECES):
         with jax.named_scope("w_br"):
@@ -503,7 +516,7 @@
                         ls[4 * g + k, pl.ds(lo, n), pl.ds(128 * a, 128)] = m.astype(BF)
         for d in (7, 1, 6, 2, 5, 3, 4):
             w = (z + d) % 8
-            send(ls.at[w, pl.ds(lo, n)], lb.at[z, pl.ds(lo, n)], q_ss.at[h, d], q_rs.at[h, d], {"z": w})
+            send(ls.at[w, pl.ds(lo, n)], lb.at[z, pl.ds(lo, n)], fin.at[9], q_rs.at[h, d], {"z": w})
         if h == 0:
             lt[...] = jnp.zeros_like(lt)
 
@@ -525,7 +538,7 @@
         return 0
 
     lax.fori_loop(0, 7, lad_step, 0)
-    send(lt, ltr, m_ss.at[6], m_rs.at[6], sib)
+    send(lt, ltr, fin.at[10], m_rs.at[6], sib)
     ea = pltpu.roll(er[...], (1280 - 75 * v) % 1280, 1)[:, :128].T[:75, 0:1]
     with jax.named_scope("w_ltr"):
         got(ltr, m_rs.at[6])
@@ -546,13 +559,13 @@
     def la_send(s, blk, d, ch):
         p = la_part(blk, c, 16 * ch)
         dev = {"z": ((zp, zm)[d] if s < 3 else (z + (2, 6)[d]) % 8)}
-        send(p, p, g_ss.at[2 * s + d, ch], g_rs.at[2 * s + d, ch], dev)
+        send(p, p, fin.at[13], g_rs.at[2 * s + d, ch], dev)
 
     HALF = ((0, 48), (48, 32))
 
     def la_push(n, blk, h):
         p = la_part(blk, c, *HALF[h])
-        send(p, p, h_ss.at[n, h], h_rs.at[n, h], sib)
+        send(p, p, fin.at[14], h_rs.at[n, h], sib)
 
     for ch in range(5):
         for d in range(2):
@@ -572,7 +585,7 @@
     sc[...] = jnp.full((8, 128), jnp.sum(total), F32)
 
     def give_sum(j, _):
-        send(sc, sp.at[v], m_ss.at[7], m_rs.at[7], plane_dev(j, c))
+        send(sc, sp.at[v], fin.at[11], m_rs.at[7], plane_dev(j, c))
         return 0
 
     lax.fori_loop(1, 16, give_sum, 0)
@@ -616,7 +629,7 @@
             sz[z] = s_all
 
             def give_sz(j, _):
-                send(sz.at[z], sz.at[z], m_ss.at[8], m_rs.at[8], {"z": (z + j) % 8})
+                send(sz.at[z], sz.at[z], fin.at[12], m_rs.at[8], {"z": (z + j) % 8})
                 return 0
 
             lax.fori_loop(1, 8, give_sz, 0)
@@ -651,68 +664,13 @@
         for o in outs:
             o.wait()
 
-    for s in range(4):
-        for d in range(2):
-            i = 2 * s + d
-            if s < 3:
-                left(rows(0, 0, 32, 512 if d else 384), r_ss.at[i])
-                left(rows(0, 0, 32, 384 if d else 512), r_ss.at[8 + i])
-                left(tt.at[0], t_ss.at[i])
-                for ch in range(5):
-                    left(la_part(0, 0, 0), g_ss.at[i, ch])
-            else:
-                left(rows(0, 0, 32), r_ss.at[i])
-                left(tt.at[0, pl.ds(0, 48 - 16 * d)], t_ss.at[i])
-                for ch in ((0, 1, 2), (3, 4))[d]:
-                    left(la_part(0, 0, 0), g_ss.at[i, ch])
-    for n in range(8):
-        left(tt.at[0], u_ss.at[n])
-    for n in range(7):
-        for ch in range(2):
-            left(la_part(0, 0, *HALF[ch]), h_ss.at[n, ch])
-    for n in (0, 1):
-        left(rows(0, 0, 16), c_ss.at[n])
-        left(xb.at[0, pl.ds(0, 16), pl.ds(0, 256)], c_ss.at[2 + n])
-        left(rows(0, 0, 64), c_ss.at[4 + n])
-        left(rows(0, 0, 32), c_ss.at[6 + n])
-        for g in range(4):
-            for q in range(4):
-                left(rows(0, 0, 96 if g < 3 else 32), e_ss.at[g, q, n])
-
-    def drain(k, wa, wb):
-        for o, w in ((0, wa), (8, wb)):
-            for n, cnt in ((0, 32), (2, 16), (4, 128), (6, 64)):
-                left(rows(0, 0, cnt, w), x_ss.at[k, o + n])
-                left(rows(0, 0, cnt, w), x_ss.at[k, o + n + 1])
-
-    def drain_two(n, _):
-        drain(2 * n + 1, 512, 384)
-        drain(2 * n + 2, 384, 512)
-        return 0
-
-    drain(0, 512, 512)
-    lax.fori_loop(0, 3, drain_two, 0)
-    drain(7, 512, 512)
-
-    @pl.when(c == y % 2)
-    def _():
-        left(zt_ref.at[pl.ds(0, 480)], m_ss.at[0])
-
-    @pl.when(c != y % 2)
-    def _():
-        left(zt_ref, m_ss.at[0])
-
-    left(hs.at[pl.ds(0, 15)], m_ss.at[1])
-    left(hb.at[0], m_ss.at[2])
-    for h in range(3):
-        left(rb.at[:, REGION[h]], d_ss.at[h])
-    for h, (lo, n) in enumerate(PIECES):
-        left(bs.at[pl.ds(0, 15), pl.ds(lo, n)], p_ss.at[h])
-        for d in range(1, 8):
-            left(ls.at[0, pl.ds(lo, n)], q_ss.at[h, d])
-    left(lt, m_ss.at[6])
-    left(sp.at[pl.ds(0, 15)], m_ss.at[7])
-    left(sz.at[pl.ds(0, 7)], m_ss.at[8])
+    left(bs.at[pl.ds(0, 15)], fin.at[8])
+    left(ls.at[pl.ds(0, 7)], fin.at[9])
+    left(lt, fin.at[10])
+    left(sp.at[pl.ds(0, 15)], fin.at[11])
+    left(sz.at[pl.ds(0, 7)], fin.at[12])
+    left(la.at[pl.ds(0, 7), :, pl.ds(0, 640)], fin.at[13])
+    left(la.at[pl.ds(0, 7), :, pl.ds(0, 640)], fin.at[14])
 
 
 def shards(amplitudes, factors, kernel, other_terms, virt_energy, pair_energy):
@@ -762,18 +720,18 @@
             V((8, 128), F32),
             V((16, 8, 128), F32),
             V((8, 8, 128), F32),
-            dma((8, 16)), dma((8, 16)),
-            dma((4, 4, 2)), dma((4, 4, 2)),
-            dma((8,)), dma((8,)),
-            dma((16,)), dma((16,)),
-            dma((8,)), dma((8,)),
-            dma((8,)), dma((8,)),
-            dma((8, 5)), dma((8, 5)),
-            dma((8, 2)), dma((8, 2)),
-            dma((16,)), dma((16,)),
-            dma((3,)), dma((3,)),
-            dma((3,)), dma((3,)),
-            dma((3, 8)), dma((3, 8)),
+            dma((8, 2)), dma((8, 8)), dma((16,)),
+            dma((4, 4, 2)),
+            dma((8,)),
+            dma((16,)),
+            dma((8,)),
+            dma((8,)),
+            dma((8, 5)),
+            dma((8, 2)),
+            dma((16,)),
+            dma((3,)),
+            dma((3,)),
+            dma((3, 8)),
             dma((12,)),
         ],
         compiler_params=pltpu.CompilerParams(

time: 130 us -> 126 us (0.969)
  Pallas kernels: 124 us -> 121 us
    pallas_call x1, Pallas kernels: 124 us -> 121 us  [shards(): pl.pallas_call(ladder_kernel, out_shape=(jax.ShapeDtypeStruct((600, 1200)...]
where the time goes in v6:
time: 126 us
  Pallas kernels  121 us (96%)
  other arithmetic  3.32 us (3%)
  between operations  2.39 us (2%)
    pallas_call x1, Pallas kernels, shards(): pl.pallas_call(ladder_kernel, out_shape=(jax.ShapeDtypeStruct((600, 1200)...  121 us
    transpose x1, other arithmetic, shards(): jnp.transpose(residual.reshape(75, 8, 1200), (1, 0, 2))  3.32 us

profile of v6, /device:TPU:1, one launch (start us, length us, event | category | flops | bytes accessed | tf_op | source)
XLA Modules:
  0.0 126.3 jit_solution(13662882958398763720)
XLA Ops:
  0.6 0.0 copy-start
  0.6 120.6 %ladder.1 = (bf16[600,1200]{1,0:T(8,128)(2,1)}, f32[1,1]{1,0:T(1,128)}) custom-call(bf16[75,512]{1,0:T(8,128)(2,1)} %f_hbm.1, bf16[600,75]{1,0:T(8,128)(2,1)} %bitcast.13, bf16[512,512]{1,0:T(8,128)(2,1)} %k_hbm.1, f32[600,1200]{1,0:T(8,128)} %bitcast.12, f32[1200]{0:T(1024)} %e_hbm.1, f32[8]{0:T(128)} %ep_hbm.1), custom_call_target="tpu_custom_call" | custom-call | tf_op jit(solution)/shard_map/ladder/pallas_call | solution.py:682
  121.2 0.0 copy-done
  121.2 3.3 %add_bitcast_fusion = f32[8,75,1200]{2,0,1:T(8,128)} fusion(bf16[600,1200]{1,0:T(8,128)(2,1)} %get-tuple-element.4, f32[8,75,1200]{2,0,1:T(8,128)S(1)} %copy-done), kind=kLoop, calls=%fused_computation | loop fusion | flops 1440000 | bytes 7200000 | tf_op jit(solution)/shard_map/transpose | solution.py:743
Async XLA Ops:
  0.6 120.6 %copy-start = (f32[8,75,1200]{2,0,1:T(8,128)S(1)}, f32[8,75,1200]{2,0,1:T(8,128)}, u32[]{:S(2)}) copy-start(f32[8,75,1200]{2,0,1:T(8,128)} %param.9) | copy-start | bytes 8640004
